TPU v7x, 32 devices: a whole 2x2x4 slice. The times are simulated.
32 devices in a mesh: expert: 4 (over z), dp: 8 (over y, x, core).
Axes of the slice: x: 2, y: 2, z: 4, core: 2. Of those that a mesh axis runs over, the one named last changes fastest.
Arguments:
- tokens: bfloat16 [4096, 2048], P(('expert', 'dp')), may hold values from -6 to 6
- cotangent: bfloat16 [4096, 2048], P(('expert', 'dp')), may hold values from -1.796875 to 1.796875
- routes: int32 [4096, 8], P(('expert', 'dp')), may hold values from 0 to 127, as said below
- probs: float32 [4096, 8], P(('expert', 'dp')), may hold values from 0.05 to 0.5
- replicas: bfloat16 [4, 8, 2048, 1152], P('expert', 'dp'), as said below
- hold_now: int32 [4, 8], replicated, may hold values from 0 to 7, as said below
- hold_next: int32 [4, 8], replicated, may hold values from 0 to 7, as said below
- master: float32 [4, 2048, 2, 1152], P('expert', 'dp'), may hold values from -0.18 to 0.18
- moment: float32 [4, 2048, 2, 1152], P('expert', 'dp'), may hold values from -1.8 to 1.8
- second: float32 [4, 2048, 2, 1152], P('expert', 'dp'), may hold values from 0.01 to 1
Outputs:
- master_out: float32 [4, 2048, 2, 1152], P('expert', 'dp')
- moment_out: float32 [4, 2048, 2, 1152], P('expert', 'dp')
- second_out: float32 [4, 2048, 2, 1152], P('expert', 'dp')
- next_replicas: bfloat16 [4, 8, 2048, 1152], P('expert', 'dp')
Inputs may be any that keep to these rules, and one draw needn't show every extreme that they name: `routes`: each token names 8 different experts of the layer; in every block of 128 tokens some expert of the window is named by at least 24 tokens. `hold_now`: slice 2 e + h is half h of window expert e; every slice is held by at least 2 devices, and some slice by exactly 2. `hold_next`: slice 2 e + h is half h of window expert e. replicas[a, j] holds slice hold_now[a, j]; devices that hold the same slice hold equal values.
All inputs are finite; a program needn't handle non-finite values.
Results may differ from a plain program's by a relative error of at most 0.001.
Values may be sent and summed in bfloat16 or wider, within the bound.
No kernel may reach another device: no remote copies, remote signals or barrier semaphores. Data moves between devices by JAX's collectives and lax.ppermute only.
A program may use at most 128 MiB of HBM per device.

v0:
```python
import functools

import jax
import jax.numpy as jnp
from jax import lax
from jax.experimental import pallas as pl
from jax.experimental.pallas import tpu as pltpu
from jax.sharding import PartitionSpec as P


CAP = 24

beta_one = 0.9
beta_two = 0.999
learn_rate = 0.01
decay_rate = 0.1
adam_eps = 1e-08
adam_count = 20.0

VMEM_LIMIT = 60 * 1024 * 1024


def adam_step(master, moment, second, gradient):
    moment_out = beta_one * moment + (1.0 - beta_one) * gradient
    second_out = beta_two * second + (1.0 - beta_two) * gradient * gradient
    scale_one = 1.0 - beta_one**adam_count
    scale_two = 1.0 - beta_two**adam_count
    update = moment_out / scale_one / (jnp.sqrt(second_out / scale_two) + adam_eps)
    master_out = master - learn_rate * (update + decay_rate * master)
    return (master_out, moment_out, second_out)


def keep_kernel(count, place_ref, routes_ref, probs_ref, tokens_ref, cot_ref, *out_refs):
    token_count = tokens_ref.shape[0]
    routes = routes_ref[...]
    probs = probs_ref[...]
    members = []
    factors = []
    for step in range(count):
        expert = lax.rem(place_ref[0] + step, count)
        picked = routes == expert
        members.append(jnp.sum(jnp.where(picked, 1.0, 0.0), axis=0, keepdims=True))
        factors.append(jnp.sum(jnp.where(picked, probs, 0.0), axis=0, keepdims=True))
    table = jnp.concatenate(members + [jnp.zeros_like(members[0])] * (-count % 8), axis=0)
    earlier = lax.broadcasted_iota(jnp.int32, (token_count, token_count), 0)
    later = lax.broadcasted_iota(jnp.int32, (token_count, token_count), 1)
    before = jnp.where(earlier < later, 1.0, 0.0).astype(jnp.bfloat16)
    ranked = jnp.dot(table.astype(jnp.bfloat16), before, preferred_element_type=jnp.float32)
    slots = lax.broadcasted_iota(jnp.int32, (CAP, token_count), 0).astype(jnp.float32)
    hits = []
    scales = []
    for step in range(count):
        hit = (members[step] > 0.5) & (ranked[step : step + 1] == slots)
        hits.append(jnp.where(hit, 1.0, 0.0))
        scales.append(jnp.sum(jnp.where(hit, factors[step], 0.0), axis=1, keepdims=True))
    one_hot = jnp.concatenate(hits, axis=0).astype(jnp.bfloat16)
    scale = jnp.concatenate(scales, axis=0)
    rows_in = jnp.dot(one_hot, tokens_ref[...], preferred_element_type=jnp.float32)
    rows_out = scale * jnp.dot(one_hot, cot_ref[...], preferred_element_type=jnp.float32)
    for step in range(count):
        span = slice(step * CAP, (step + 1) * CAP)
        out_refs[step][0] = rows_in[span].astype(jnp.bfloat16)
        out_refs[step][1] = rows_out[span].astype(jnp.bfloat16)


def keep_rows(tokens, cotangent, routes, probs, place, count):
    width = tokens.shape[1]
    vmem = pl.BlockSpec(memory_space=pltpu.VMEM)
    return pl.pallas_call(
        functools.partial(keep_kernel, count),
        out_shape=[jax.ShapeDtypeStruct((2, CAP, width), jnp.bfloat16)] * count,
        in_specs=[pl.BlockSpec(memory_space=pltpu.SMEM)] + [vmem] * 4,
        out_specs=[vmem] * count,
        cost_estimate=pl.CostEstimate(flops=4_000_000_000, bytes_accessed=2_000_000, transcendentals=0),
        name="keep_rows",
    )(place, routes.T, probs.T, tokens, cotangent)


def turn_kernel(parts, weight_ref, out_ref):
    half_width = weight_ref.shape[1] // 3
    units = half_width // parts
    if units % 16 == 0:
        turned = weight_ref[...].T
    else:
        turned = weight_ref[...].astype(jnp.float32).T
    for piece in range(parts):
        rows = [
            turned[kind * half_width + piece * units : kind * half_width + (piece + 1) * units]
            for kind in range(3)
        ]
        out_ref[piece] = jnp.concatenate(rows, axis=0).astype(jnp.bfloat16)


def turn_weights(weight, part, parts):
    width, columns = weight.shape
    span = width // 2
    block = min(256, span)
    steps = span // block
    return pl.pallas_call(
        functools.partial(turn_kernel, parts),
        out_shape=jax.ShapeDtypeStruct((parts, columns // parts, span), jnp.bfloat16),
        grid=(steps,),
        in_specs=[pl.BlockSpec((block, columns), lambda i: (part * steps + i, 0))],
        out_specs=pl.BlockSpec((parts, columns // parts, block), lambda i: (0, 0, i)),
        cost_estimate=pl.CostEstimate(flops=4_000_000_000, bytes_accessed=5_000_000, transcendentals=0),
        name="turn_weights",
    )(weight)


def grad_kernel(count, chunks, table_ref, own0_ref, own1_ref, far_ref, *refs):
    ins = refs[:count]
    outs = refs[count : 2 * count]
    grads = refs[2 * count : 2 * count + chunks]
    rows_in, rows_out, pair_w, down_w, pair_g, down_g, sems = refs[2 * count + chunks :]
    rows = ins[0].shape[0]
    units = down_w.shape[0] // 2
    span = own0_ref.shape[2]
    own_refs = (own0_ref, own1_ref)
    width = rows_in.shape[1]

    copies = []
    for index in range(count):
        place = pl.ds(index * rows, rows)
        copies.append(pltpu.make_async_copy(ins[index], rows_in.at[place], sems.at[0, index]))
        copies.append(pltpu.make_async_copy(outs[index], rows_out.at[place], sems.at[1, index]))
    for copy in copies:
        copy.start()

    for unit in range(4):
        half, part = unit // 2, unit % 2
        lanes = pl.ds(part * span, span)

        def fetch(source, unit=unit, half=half, lanes=lanes):
            one = pltpu.make_async_copy(
                source.at[pl.ds(0, 2 * units)],
                pair_w.at[pl.ds(2 * half * units, 2 * units), lanes],
                sems.at[2, 2 * unit],
            )
            two = pltpu.make_async_copy(
                source.at[pl.ds(2 * units, units)],
                down_w.at[pl.ds(half * units, units), lanes],
                sems.at[2, 2 * unit + 1],
            )
            one.start()
            two.start()
            one.wait()
            two.wait()

        @pl.when(table_ref[0, half] == 0)
        def _(half=half, part=part, fetch=fetch):
            fetch(own_refs[part].at[table_ref[1, half]])

        @pl.when(table_ref[0, half] != 0)
        def _(half=half, part=part, fetch=fetch):
            fetch(far_ref.at[half, part])

    for copy in copies:
        copy.wait()

    contract = (((1,), (1,)), ((), ()))
    pair = lax.dot_general(pair_w[...], rows_in[...], contract, preferred_element_type=jnp.float32)
    down = lax.dot_general(down_w[...], rows_out[...], contract, preferred_element_type=jnp.float32)
    for half in range(2):
        gate = pair[2 * half * units : (2 * half + 1) * units]
        up = pair[(2 * half + 1) * units : (2 * half + 2) * units]
        hidden_grad = down[half * units : (half + 1) * units]
        sig = jax.nn.sigmoid(gate)
        activated = gate * sig
        down_g[pl.ds(half * units, units)] = (activated * up).astype(jnp.bfloat16)
        gate_grad = hidden_grad * up * sig * (1.0 + gate * (1.0 - sig))
        pair_g[pl.ds(2 * half * units, 2 * units)] = jnp.concatenate(
            [gate_grad, hidden_grad * activated], axis=0
        ).astype(jnp.bfloat16)

    owners = grads[0].shape[0]
    block = width // owners
    lane = block // chunks

    def owner_step(owner, carry):
        place = pl.ds(pl.multiple_of(owner * block, block), block)
        grad_in = jnp.dot(pair_g[...], rows_in[:, place], preferred_element_type=jnp.float32)
        grad_out = jnp.dot(down_g[...], rows_out[:, place], preferred_element_type=jnp.float32)
        for chunk in range(chunks):
            part = slice(chunk * lane, (chunk + 1) * lane)
            for half in range(2):
                grads[chunk][owner, pl.ds(3 * half * units, 2 * units)] = grad_in[
                    2 * half * units : (2 * half + 2) * units, part
                ]
                grads[chunk][owner, pl.ds((3 * half + 2) * units, units)] = grad_out[
                    half * units : (half + 1) * units, part
                ]
        return carry

    lax.fori_loop(0, owners, owner_step, 0)


def half_grads(table, own, far, ins, outs, owners, chunks):
    count = len(ins)
    rows, width = ins[0].shape
    units = own[0].shape[1] // 3
    tokens = count * rows
    anywhere = pl.BlockSpec(memory_space=pl.ANY)
    lane = width // owners // chunks
    return pl.pallas_call(
        functools.partial(grad_kernel, count, chunks),
        out_shape=[jax.ShapeDtypeStruct((owners, 6 * units, lane), jnp.float32)] * chunks,
        in_specs=[pl.BlockSpec(memory_space=pltpu.SMEM)] + [anywhere] * (3 + 2 * count),
        out_specs=[pl.BlockSpec(memory_space=pltpu.VMEM)] * chunks,
        scratch_shapes=[
            pltpu.VMEM((tokens, width), jnp.bfloat16),
            pltpu.VMEM((tokens, width), jnp.bfloat16),
            pltpu.VMEM((4 * units, width), jnp.bfloat16),
            pltpu.VMEM((2 * units, width), jnp.bfloat16),
            pltpu.VMEM((4 * units, tokens), jnp.bfloat16),
            pltpu.VMEM((2 * units, tokens), jnp.bfloat16),
            pltpu.SemaphoreType.DMA((3, max(8, count))),
        ],
        compiler_params=pltpu.CompilerParams(vmem_limit_bytes=VMEM_LIMIT),
        cost_estimate=pl.CostEstimate(flops=10_000_000_000, bytes_accessed=10_000_000, transcendentals=0),
        name="half_grads",
    )(table, *own, far, *ins, *outs)


def update_kernel(sizes, held, arrived_ref, master_ref, moment_ref, second_ref, *out_refs):
    out_refs = out_refs[held:]
    parts, lines, _ = arrived_ref.shape
    units = lines // 6
    master_out, moment_out, second_out = out_refs[:3]
    fresh_refs = out_refs[3:]
    for half in range(2):
        stacked = jnp.concatenate(
            [
                arrived_ref[part, pl.ds((3 * half + kind) * units, units)]
                for kind in range(3)
                for part in range(parts)
            ],
            axis=0,
        )
        master, moment, second = adam_step(
            master_ref[half], moment_ref[half], second_ref[half], stacked.T
        )
        master_out[half] = master
        moment_out[half] = moment
        second_out[half] = second
        fresh = master.astype(jnp.bfloat16)
        begin = 0
        for index, size in enumerate(sizes):
            fresh_refs[2 * index + half][...] = fresh[begin : begin + size]
            begin += size


def update_rows(arrived, master, moment, second, chunk, sizes, held):
    lane = arrived.shape[2]
    columns = master.shape[2]
    state = pl.BlockSpec((2, lane, columns), lambda i: (0, chunk, 0))
    pieces = [size for size in sizes for _ in range(2)]
    return pl.pallas_call(
        functools.partial(update_kernel, sizes, len(held)),
        grid=(1,),
        out_shape=[jax.ShapeDtypeStruct(master.shape, jnp.float32)] * 3
        + [jax.ShapeDtypeStruct((size, columns), jnp.bfloat16) for size in pieces],
        in_specs=[pl.BlockSpec(arrived.shape, lambda i: (0, 0, 0)), state, state, state]
        + [pl.BlockSpec(memory_space=pl.ANY)] * len(held),
        out_specs=[state] * 3 + [pl.BlockSpec((size, columns), lambda i: (0, 0)) for size in pieces],
        input_output_aliases={4 + index: index for index in range(len(held))},
        compiler_params=pltpu.CompilerParams(vmem_limit_bytes=VMEM_LIMIT),
        cost_estimate=pl.CostEstimate(flops=4_000_000_000, bytes_accessed=9_000_000, transcendentals=0),
        name="update_rows",
    )(arrived, master, moment, second, *held)


def choose_kernel(count, want_ref, *refs):
    sources = refs[:count]
    out_ref = refs[count]
    for slot in range(out_ref.shape[0]):
        for index in range(count):

            @pl.when(want_ref[slot] == index)
            def _(slot=slot, index=index):
                out_ref[slot] = sources[index][...]


def choose_pieces(want, sources):
    count = len(sources)
    slots = want.shape[0]
    rows, columns = sources[0].shape
    vmem = pl.BlockSpec(memory_space=pltpu.VMEM)
    return pl.pallas_call(
        functools.partial(choose_kernel, count),
        out_shape=jax.ShapeDtypeStruct((slots, rows, columns), sources[0].dtype),
        in_specs=[pl.BlockSpec(memory_space=pltpu.SMEM)] + [vmem] * count,
        out_specs=vmem,
        compiler_params=pltpu.CompilerParams(vmem_limit_bytes=VMEM_LIMIT),
        cost_estimate=pl.CostEstimate(flops=1_500_000_000, bytes_accessed=4_000_000, transcendentals=0),
        name="choose_pieces",
    )(want, *sources)


def swap(value, mask, count):
    return lax.ppermute(value, "dp", [(i, i ^ mask) for i in range(count)])


def gather_rows(pieces, count):
    masks = [1 << bit for bit in range(count.bit_length() - 1)]
    while len(masks) >= 2:
        two, one = masks.pop(), masks.pop()
        grown = []
        for piece in pieces:
            first = [swap(half, one, count) for half in piece]
            other = [swap(half, two, count) for half in piece]
            far = (swap(first[0], two, count), swap(other[1], one, count))
            grown += [piece, tuple(first), tuple(other), far]
        pieces = grown
    if masks:
        pieces = pieces + [tuple(swap(half, masks[0], count) for half in piece) for piece in pieces]
    return pieces


def step_body(tokens, cotangent, routes, probs, replicas, hold_now, hold_next, master, moment, second):
    planes = lax.axis_size("expert")
    columns = lax.axis_size("dp")
    devices = planes * columns
    width = tokens.shape[1]
    block_rows = width // columns
    plane = lax.axis_index("expert")

    kept = keep_rows(tokens, cotangent, routes, probs, plane.reshape(1), planes)
    came = [kept[0]] + [
        lax.ppermute(kept[step], "expert", [(i, (i + step) % planes) for i in range(planes)])
        for step in range(1, planes)
    ]

    flat = hold_now.reshape(devices)
    ids = jnp.arange(devices, dtype=jnp.int32)
    pieces_ids = jnp.arange(2 * planes, dtype=jnp.int32)
    apart = jnp.abs(ids[None, :] // columns - pieces_ids[:, None] // 2)
    order = jnp.where(flat[None, :] == pieces_ids[:, None], apart * devices + ids[None, :], devices * devices)
    holder = jnp.min(order, axis=1) % devices
    from_plane = (holder // columns).reshape(planes, 2)
    from_column = (holder % columns).reshape(planes, 2)
    shift = jnp.arange(planes, dtype=jnp.int32)[:, None] - from_plane

    own = []
    for part in range(2):
        turned = turn_weights(replicas[0, 0], part, columns)
        own.append(lax.all_to_all(turned, "dp", split_axis=0, concat_axis=0, tiled=True))
    own = tuple(own)

    first = (
        jnp.concatenate([rows[0] for rows in came], axis=0),
        jnp.concatenate([rows[1] for rows in came], axis=0),
    )
    state = tuple(jnp.transpose(part[0], (1, 0, 2)) for part in (master, moment, second))
    (first, own, state) = lax.optimization_barrier((first, own, state))
    signs = jnp.array([1, -1], jnp.int32)[:, None, None]
    steps = jnp.arange(1, planes, dtype=jnp.int32)[None, :, None]
    experts = jnp.arange(planes, dtype=jnp.int32)
    needs = shift[None, None] == (signs * steps)[..., None]
    trips = jnp.max(jnp.sum(needs.astype(jnp.int32), axis=3), axis=(0, 2))
    reached = (experts[None, None, :] == plane + signs * steps)[..., None]
    need_there = jnp.any(needs & reached, axis=2)
    column_there = jnp.sum(jnp.where(reached, from_column[None, None], 0), axis=2)
    send_column = jnp.stack(
        [jnp.where(need_there[..., 0], column_there[..., 0], column_there[..., 1]), column_there[..., 1]],
        axis=2,
    )
    here = (experts == plane)[:, None]
    need_here = jnp.any(needs & here[None, None], axis=2)
    first_here, last_here = need_here[..., 0], need_here[..., 1]
    none_here = jnp.zeros_like(first_here)
    takes = jnp.stack(
        [
            jnp.stack([first_here, last_here & ~first_here], axis=2),
            jnp.stack([none_here, last_here & first_here], axis=2),
        ],
        axis=2,
    )
    side = jnp.any(jnp.where(here, shift, 0) != 0, axis=0).astype(jnp.int32)
    table = jnp.stack([side, jnp.sum(jnp.where(here, from_column, 0), axis=0)])

    far = jnp.zeros((2, 2) + own[0].shape[1:], own[0].dtype)
    for step in range(1, planes):

        def trip(index, kept_far, step=step):
            for sign_index, sign in enumerate((1, -1)):
                source = send_column[sign_index, step - 1, index]
                pairs = [(i, i + sign * step) for i in range(planes) if 0 <= i + sign * step < planes]
                sent = jnp.stack(
                    [lax.dynamic_index_in_dim(part, source, 0, keepdims=False) for part in own]
                )
                got = lax.ppermute(sent, "expert", pairs)
                take = takes[sign_index, step - 1, index]
                kept_far = jnp.where(take[:, None, None, None], got[None], kept_far)
            return kept_far

        far = lax.fori_loop(0, trips[step - 1], trip, far)

    rows = gather_rows([first], columns)

    chunks = max(1, block_rows // 128)
    partial = half_grads(
        table, own, far, [r[0] for r in rows], [r[1] for r in rows], columns, chunks
    )
    lane = block_rows // chunks
    updated = []
    fresh = []
    for chunk in range(chunks):
        arrived = lax.all_to_all(partial[chunk], "dp", split_axis=0, concat_axis=0, tiled=True)
        cut = lane * 5 // 8 // 16 * 16
        sizes = [lane] if chunk + 1 < chunks or cut == 0 else [cut, lane - cut]
        result = update_rows(arrived, *state, chunk, sizes, updated)
        updated = result[:3]
        fresh += [(result[3 + 2 * i], result[4 + 2 * i]) for i in range(len(sizes))]

    next_row = lax.dynamic_index_in_dim(hold_next, plane, 0, keepdims=False)
    next_plane = next_row // 2
    next_half = next_row % 2
    turns = jnp.where(next_half == 0, plane - next_plane, next_plane - plane)
    want = (next_half * planes + (turns + planes) % planes).astype(jnp.int32)
    forward = [(i, (i + 1) % planes) for i in range(planes)]
    backward = [(i, (i - 1) % planes) for i in range(planes)]
    outs = []
    for kind in range(3):
        out = jnp.transpose(updated[kind], (1, 0, 2))[None]
        outs.append(out)
    replica = None
    begin = 0
    for own_halves in fresh:
        rings = [[own_halves[0]], [own_halves[1]]]
        for _ in range(1, planes):
            rings[0].append(lax.ppermute(rings[0][-1], "expert", forward))
            rings[1].append(lax.ppermute(rings[1][-1], "expert", backward))
        sources = rings[0] + rings[1]
        outgoing = choose_pieces(want, sources)
        arrived = lax.all_to_all(outgoing, "dp", split_axis=0, concat_axis=0, tiled=True)
        if replica is None:
            replica = jnp.zeros((columns, block_rows, arrived.shape[2]), arrived.dtype)
        replica = lax.dynamic_update_slice(replica, arrived, (0, begin, 0))
        begin += own_halves[0].shape[0]
    next_replicas = replica.reshape(1, 1, width, replica.shape[2])

    return (*outs, next_replicas)


def solution(mesh):
    placed = (
        P(("expert", "dp"), None),
        P(("expert", "dp"), None),
        P(("expert", "dp"), None),
        P(("expert", "dp"), None),
        P("expert", "dp", None, None),
        P(),
        P(),
        P("expert", "dp", None, None),
        P("expert", "dp", None, None),
        P("expert", "dp", None, None),
    )
    return jax.shard_map(
        step_body,
        mesh=mesh,
        in_specs=placed,
        out_specs=(P("expert", "dp", None, None),) * 4,
        check_vma=False,
    )
```

profile of v0, /device:TPU:0, one launch (start us, length us, event | category | flops | bytes accessed | tf_op | source)
XLA Modules:
  0.0 363.1 jit_solution(7910983484184040967)
XLA Ops:
  0.6 2.6 keep_rows.1
  3.2 3.0 collective-permute-start.6
  6.3 2.6 collective-permute-start.7
  10.2 4.2 %turn_weights.3 = bf16[8,144,1024]{2,1,0:T(8,128)(2,1)} custom-call(bf16[2048,1152]{1,0:T(8,128)(2,1)} %bitcast.101), custom_call_target="tpu_custom_call" | custom-call | flops 4000000000 | bytes 5000000 | tf_op jit(solution)/shard_map/turn_weights/pallas_call | solution.py:99
  14.4 3.9 %all-to-all-start.1 = ((bf16[8,144,1024]{2,1,0:T(8,128)(2,1)}), bf16[8,144,1024]{2,1,0:T(8,128)(2,1)S(1)}, u32[]{:S(2)}, u32[]{:S(2)}) async-start(bf16[8,144,1024]{2,1,0:T(8,128)(2,1)} %turn_weights.3), calls=%async_computation.1 | async-start | bytes 4718592 | tf_op jit(solution)/shard_map/all_to_all | solution.py:346
  20.8 3.2 copy.69
  24.3 4.2 %turn_weights.2 = bf16[8,144,1024]{2,1,0:T(8,128)(2,1)} custom-call(bf16[2048,1152]{1,0:T(8,128)(2,1)} %bitcast.102), custom_call_target="tpu_custom_call" | custom-call | flops 4000000000 | bytes 5000000 | tf_op jit(solution)/shard_map/turn_weights/pallas_call | solution.py:99
  28.5 4.8 %copy_bitcast_fusion = (f32[2,256,1152]{2,1,0:T(8,128)}, f32[2,256,1152]{2,1,0:T(8,128)}) fusion(f32[1,256,2,1152]{3,2,1,0:T(2,128)} %param.26, f32[1,256,2,1152]{3,2,1,0:T(2,128)} %param.25), kind=kLoop, calls=%fused_computation.35 | loop fusion | bytes 9437184 | tf_op jit(solution)/shard_map/transpose | solution.py:353
  33.3 14.4 %all-to-all-done.1.own1_ref = bf16[8,144,1024]{2,1,0:T(8,128)(2,1)S(1)} async-done(((bf16[8,144,1024]{2,1,0:T(8,128)(2,1)}), bf16[8,144,1024]{2,1,0:T(8,128)(2,1)S(1)}, u32[]{:S(2)}, u32[]{:S(2)}) %all-to-all-start.1) | async-done | bytes 2359328 | tf_op jit(solution)/shard_map/all_to_all | solution.py:346
  47.7 4.4 %all-to-all-start = ((bf16[8,144,1024]{2,1,0:T(8,128)(2,1)}), bf16[8,144,1024]{2,1,0:T(8,128)(2,1)}, u32[]{:S(2)}, u32[]{:S(2)}) async-start(bf16[8,144,1024]{2,1,0:T(8,128)(2,1)} %turn_weights.2), calls=%async_computation | async-start | bytes 4718592 | tf_op jit(solution)/shard_map/all_to_all | solution.py:346
  53.8 27.7 %all-to-all-done.own0_ref = bf16[8,144,1024]{2,1,0:T(8,128)(2,1)} async-done(((bf16[8,144,1024]{2,1,0:T(8,128)(2,1)}), bf16[8,144,1024]{2,1,0:T(8,128)(2,1)}, u32[]{:S(2)}, u32[]{:S(2)}) %all-to-all-start) | async-done | bytes 2359328 | tf_op jit(solution)/shard_map/all_to_all | solution.py:346
  82.8 56.7 %while.30 = (s32[]{:T(128)}, bf16[2,2,144,1024]{3,2,1,0:T(8,128)(2,1)S(1)}, s32[]{:T(128)}, pred[2,3,2,2]{3,2,1,0:T(4,128)(4,1)S(1)}, s32[2,3,2]{1,2,0:T(2,128)S...) while((s32[]{:T(128)}, ...), condition=%wide.region_9.10_spmd, body=%wide.region_8.9_spmd.sunk | while | flops 1769483 | bytes 12976463 | solution.py:396
  92.1 5.4 %collective-permute-start = (bf16[2,144,1024]{2,1,0:T(8,128)(2,1)}, bf16[2,144,1024]{2,1,0:T(8,128)(2,1)}, u32[]{:S(2)}, u32[]{:S(2)}) collective-permute-start(bf16[2,144,1024]{2,1,0:T(8,128)(2,1)} %pad_maximum_fusion.14), channel_id=1, source_target_pairs={{0,8},{8,16},{16,24},{1,9},{9,17},{17,25},{2,10},{10,18},{18,26},{... | collective-permute-start | bytes 1769480 | tf_op jit(solution)/shard_map/while/body/ppermute | solution.py:391
  97.4 9.8 %collective-permute-done.1 = bf16[2,144,1024]{2,1,0:T(8,128)(2,1)} collective-permute-done((bf16[2,144,1024]{2,1,0:T(8,128)(2,1)}, bf16[2,144,1024]{2,1,0:T(8,128)(2,1)}, u32[]{:S(2)}, u32[]{:S(2)}) %collective-permute-start.1) | collective-permute-done | bytes 589856 | tf_op jit(solution)/shard_map/while/body/ppermute | solution.py:391
  107.3 2.0 collective-permute-done
  109.3 1.7 select_select_fusion.6
  120.3 5.8 %collective-permute-start = (bf16[2,144,1024]{2,1,0:T(8,128)(2,1)}, bf16[2,144,1024]{2,1,0:T(8,128)(2,1)}, u32[]{:S(2)}, u32[]{:S(2)}) collective-permute-start(bf16[2,144,1024]{2,1,0:T(8,128)(2,1)} %pad_maximum_fusion.14), channel_id=1, source_target_pairs={{0,8},{8,16},{16,24},{1,9},{9,17},{17,25},{2,10},{10,18},{18,26},{... | collective-permute-start | bytes 1769480 | tf_op jit(solution)/shard_map/while/body/ppermute | solution.py:391
  126.1 9.0 %collective-permute-done.1 = bf16[2,144,1024]{2,1,0:T(8,128)(2,1)} collective-permute-done((bf16[2,144,1024]{2,1,0:T(8,128)(2,1)}, bf16[2,144,1024]{2,1,0:T(8,128)(2,1)}, u32[]{:S(2)}, u32[]{:S(2)}) %collective-permute-start.1) | collective-permute-done | bytes 589856 | tf_op jit(solution)/shard_map/while/body/ppermute | solution.py:391
  135.1 2.0 collective-permute-done
  137.1 1.7 select_select_fusion.6
  140.8 1.4 collective-permute-start.17
  142.2 1.6 collective-permute-start.16
  144.6 8.5 %collective-permute-done.17.refs_10_ = bf16[96,2048]{1,0:T(8,128)(2,1)S(1)} collective-permute-done((bf16[96,2048]{1,0:T(8,128)(2,1)}, bf16[96,2048]{1,0:T(8,128)(2,1)S(1)}, u32[]{:S(2)}, u32[]{:S(2)}) %collective-permute-start.17) | collective-permute-done | bytes 393248 | tf_op jit(solution)/shard_map/ppermute | solution.py:300
  153.1 1.5 collective-permute-start.18
  155.1 3.4 collective-permute-done.11.refs_3_
  158.5 3.9 %collective-permute-done.18.refs_11_ = bf16[96,2048]{1,0:T(8,128)(2,1)S(1)} collective-permute-done((bf16[96,2048]{1,0:T(8,128)(2,1)S(1)}, bf16[96,2048]{1,0:T(8,128)(2,1)S(1)}, u32[]{:S(2)}, u32[]{:S(2)}) %collective-permute-start.18) | collective-permute-done | bytes 393248 | tf_op jit(solution)/shard_map/ppermute | solution.py:300
  165.0 10.9 %half_grads.1 = (f32[8,288,128]{2,1,0:T(8,128)}, f32[8,288,128]{2,1,0:T(8,128)}) custom-call(s32[2,2]{1,0:T(2,128)} %pad_add_fusion.3.table_ref, bf16[8,144,1024]{2,1,0:T(8,128)(2,1)} %all-to-all-done.own0_ref, bf16[8,144,1024]{2,1,0:T(8,128)(2,1)S(1)} %get-tuple-element.629, bf16[2,2,144,1024]{3,2,1,0:T(8,128)(2,1)S(1)} %get-tuple-element.151.far_ref, ...), custom_call_target="tpu_custom_call" | custom-call | flops 10000000000 | bytes 10000000 | tf_op jit(solution)/shard_map/half_grads/pallas_call | solution.py:204
  176.0 21.0 %all_to_all.35.arrived_ref = f32[8,288,128]{2,1,0:T(8,128)} all-to-all(f32[8,288,128]{2,1,0:T(8,128)} %get-tuple-element.158), channel_id=1, replica_groups=mesh['expert'=4,'dp'=8] {'dp'}, dimensions={0} | all-to-all | bytes 2359296 | tf_op jit(solution)/shard_map/all_to_all | solution.py:408
  197.0 3.6 all-to-all-start.2
  200.5 5.4 %update_rows.2 = (f32[2,256,1152]{2,1,0:T(8,128)}, f32[2,256,1152]{2,1,0:T(8,128)}, f32[2,256,1152]{2,1,0:T(8,128)}, bf16[128,1152]{1,0:T(8,128)(2,1)}, bf16[128,1152]{1,0:T(8,128)(2,1)}) custom-call(f32[8,288,128]{2,1,0:T(8,128)} %all_to_all.35.arrived_ref, f32[2,256,1152]{2,1,0:T(8,128)} %bitcast.93, f32[2,256,1152]{2,1,0:T(8,128)} %get-tuple-element.156.moment_ref, ...), custom_call_target="tpu_custom_call" | custom-call | flops 4000000000 | bytes 9000000 | tf_op jit(solution)/shard_map/update_rows/pallas_call | solution.py:257
  205.9 11.3 %all-to-all-done.2.arrived_ref = f32[8,288,128]{2,1,0:T(8,128)S(1)} async-done(((f32[8,288,128]{2,1,0:T(8,128)}), f32[8,288,128]{2,1,0:T(8,128)S(1)}, u32[]{:S(2)}, u32[]{:S(2)}) %all-to-all-start.2) | async-done | bytes 1179680 | tf_op jit(solution)/shard_map/all_to_all | solution.py:408
  218.3 5.3 %update_rows.3 = (f32[2,256,1152]{2,1,0:T(8,128)}, f32[2,256,1152]{2,1,0:T(8,128)}, f32[2,256,1152]{2,1,0:T(8,128)}, bf16[80,1152]{1,0:T(8,128)(2,1)}, bf16[80,1...) custom-call(f32[8,288,128]{2,1,0:T(8,128)} %copy-done.4, ...), custom_call_target="tpu_custom_call", output_to_operand_aliasing={{0}: (4, {}), {1}: (5, {}), {2}: (6, {})} | custom-call | flops 4000000000 | bytes 9000000 | tf_op jit(solution)/shard_map/update_rows/pallas_call | solution.py:257
  224.9 2.5 collective-permute-start.32
  227.4 3.8 %collective-permute-done.29.refs_1_ = bf16[80,1152]{1,0:T(8,128)(2,1)S(1)} collective-permute-done((bf16[80,1152]{1,0:T(8,128)(2,1)}, bf16[80,1152]{1,0:T(8,128)(2,1)S(1)}, u32[]{:S(2)}, u32[]{:S(2)}) %collective-permute-start.29) | collective-permute-done | bytes 184352 | tf_op jit(solution)/shard_map/ppermute | solution.py:431
  231.9 4.0 %collective-permute-done.32.refs_5_ = bf16[80,1152]{1,0:T(8,128)(2,1)S(1)} collective-permute-done((bf16[80,1152]{1,0:T(8,128)(2,1)}, bf16[80,1152]{1,0:T(8,128)(2,1)S(1)}, u32[]{:S(2)}, u32[]{:S(2)}) %collective-permute-start.32) | collective-permute-done | bytes 184352 | tf_op jit(solution)/shard_map/ppermute | solution.py:432
  235.9 1.8 collective-permute-start.33
  239.0 6.7 %collective-permute-done.33.refs_6_ = bf16[80,1152]{1,0:T(8,128)(2,1)S(1)} collective-permute-done((bf16[80,1152]{1,0:T(8,128)(2,1)S(1)}, bf16[80,1152]{1,0:T(8,128)(2,1)S(1)}, u32[]{:S(2)}, u32[]{:S(2)}) %collective-permute-start.33) | collective-permute-done | bytes 184352 | tf_op jit(solution)/shard_map/ppermute | solution.py:432
  247.6 3.7 %collective-permute-done.34.refs_7_ = bf16[80,1152]{1,0:T(8,128)(2,1)S(1)} collective-permute-done((bf16[80,1152]{1,0:T(8,128)(2,1)S(1)}, bf16[80,1152]{1,0:T(8,128)(2,1)S(1)}, u32[]{:S(2)}, u32[]{:S(2)}) %collective-permute-start.34) | collective-permute-done | bytes 184352 | tf_op jit(solution)/shard_map/ppermute | solution.py:432
  252.0 3.1 choose_pieces.4
  255.1 5.1 %all-to-all-start.5 = ((bf16[8,80,1152]{2,1,0:T(8,128)(2,1)}), bf16[8,80,1152]{2,1,0:T(8,128)(2,1)S(1)}, u32[]{:S(2)}, u32[]{:S(2)}) async-start(bf16[8,80,1152]{2,1,0:T(8,128)(2,1)} %choose_pieces.4), calls=%async_computation.5 | async-start | bytes 2949120 | tf_op jit(solution)/shard_map/all_to_all | solution.py:435
  261.0 3.1 collective-permute-start.26
  264.1 7.9 %collective-permute-done.23.refs_1_ = bf16[128,1152]{1,0:T(8,128)(2,1)S(1)} collective-permute-done((bf16[128,1152]{1,0:T(8,128)(2,1)S(1)}, bf16[128,1152]{1,0:T(8,128)(2,1)S(1)}, u32[]{:S(2)}, u32[]{:S(2)}) %collective-permute-start.23) | collective-permute-done | bytes 294944 | tf_op jit(solution)/shard_map/ppermute | solution.py:431
  272.0 4.2 %collective-permute-start.24 = (bf16[128,1152]{1,0:T(8,128)(2,1)S(1)}, bf16[128,1152]{1,0:T(8,128)(2,1)S(1)}, u32[]{:S(2)}, u32[]{:S(2)}) collective-permute-start(bf16[128,1152]{1,0:T(8,128)(2,1)S(1)} %collective-permute-done.23.refs_1_), channel_id=1, source_target_pairs={{0,8},{8,16},{16,24},{24,0},{1,9},{9,17},{17,25},{25,1},{2,10},{10... | collective-permute-start | bytes 884744 | tf_op jit(solution)/shard_map/ppermute | solution.py:431
  276.6 2.5 collective-permute-start.27
  279.1 7.4 %collective-permute-done.24.refs_2_ = bf16[128,1152]{1,0:T(8,128)(2,1)S(1)} collective-permute-done((bf16[128,1152]{1,0:T(8,128)(2,1)S(1)}, bf16[128,1152]{1,0:T(8,128)(2,1)S(1)}, u32[]{:S(2)}, u32[]{:S(2)}) %collective-permute-start.24) | collective-permute-done | bytes 294944 | tf_op jit(solution)/shard_map/ppermute | solution.py:431
  286.5 4.9 %collective-permute-start.25 = (bf16[128,1152]{1,0:T(8,128)(2,1)S(1)}, bf16[128,1152]{1,0:T(8,128)(2,1)S(1)}, u32[]{:S(2)}, u32[]{:S(2)}) collective-permute-start(bf16[128,1152]{1,0:T(8,128)(2,1)S(1)} %collective-permute-done.24.refs_2_), channel_id=1, source_target_pairs={{0,8},{8,16},{16,24},{24,0},{1,9},{9,17},{17,25},{25,1},{2,10},{10... | collective-permute-start | bytes 884744 | tf_op jit(solution)/shard_map/ppermute | solution.py:431
  293.6 6.6 %collective-permute-done.25.refs_3_ = bf16[128,1152]{1,0:T(8,128)(2,1)S(1)} collective-permute-done((bf16[128,1152]{1,0:T(8,128)(2,1)S(1)}, bf16[128,1152]{1,0:T(8,128)(2,1)S(1)}, u32[]{:S(2)}, u32[]{:S(2)}) %collective-permute-start.25) | collective-permute-done | bytes 294944 | tf_op jit(solution)/shard_map/ppermute | solution.py:431
  300.2 4.3 %collective-permute-done.28.refs_7_ = bf16[128,1152]{1,0:T(8,128)(2,1)S(1)} collective-permute-done((bf16[128,1152]{1,0:T(8,128)(2,1)S(1)}, bf16[128,1152]{1,0:T(8,128)(2,1)S(1)}, u32[]{:S(2)}, u32[]{:S(2)}) %collective-permute-start.28) | collective-permute-done | bytes 294944 | tf_op jit(solution)/shard_map/ppermute | solution.py:432
  305.3 3.6 %choose_pieces.3 = bf16[8,128,1152]{2,1,0:T(8,128)(2,1)} custom-call(s32[8]{0:T(128)} %fusion.9.want_ref, bf16[128,1152]{1,0:T(8,128)(2,1)} %get-tuple-element.165.refs_0_, bf16[128,1152]{1,0:T(8,128)(2,1)} %copy-done.21, bf16[128,1152]{1,0:T(8,128)(2,1)} %copy-done.23, bf16[128,1152]{1,0:T(8,128)(2,1)} %copy-done.25, ...), custom_call_target="tpu_custom_call" | custom-call | flops 1500000000 | bytes 4000000 | tf_op jit(solution)/shard_map/choose_pieces/pallas_call | solution.py:288
  310.1 3.6 all-to-all-start.4
  314.3 3.3 collective-permute-start.38
  317.6 3.9 %collective-permute-done.35.refs_1_ = bf16[48,1152]{1,0:T(8,128)(2,1)S(1)} collective-permute-done((bf16[48,1152]{1,0:T(8,128)(2,1)S(1)}, bf16[48,1152]{1,0:T(8,128)(2,1)S(1)}, u32[]{:S(2)}, u32[]{:S(2)}) %collective-permute-start.35) | collective-permute-done | bytes 110624 | tf_op jit(solution)/shard_map/ppermute | solution.py:431
  322.4 2.9 collective-permute-start.39
  325.3 3.1 collective-permute-done.36.refs_2_
  328.4 1.5 collective-permute-start.37
  329.9 3.1 collective-permute-start.40
  333.0 2.0 collective-permute-done.37.refs_3_
  336.8 2.7 choose_pieces.5
  339.5 3.5 all-to-all-done.4
  343.0 3.6 all-to-all-start.6
  346.6 5.0 %copy.51 = f32[1,256,2,1152]{3,2,1,0:T(2,128)} copy(f32[1,256,2,1152]{3,1,2,0:T(8,128)} %bitcast.95) | data formatting | bytes 4718592
  351.7 3.2 copy.52
  354.9 3.2 copy.53
  358.1 2.8 dynamic_update_slice.9
  (184 shorter events, 39.2 us)
Async XLA Ops:
  3.2 49.6 %collective-permute-start.6 = (bf16[2,24,2048]{2,1,0:T(8,128)(2,1)}, bf16[2,24,2048]{2,1,0:T(8,128)(2,1)S(1)}, u32[]{:S(2)}, u32[]{:S(2)}) collective-permute-start(bf16[2,24,2048]{2,1,0:T(8,128)(2,1)} %get-tuple-element.144), channel_id=1, source_target_pairs={{0,8},{8,16},{16,24},{24,0},{1,9},{9,17},{17,25},{25,1},{2,10},{10... | collective-permute-start | bytes 589832 | tf_op jit(solution)/shard_map/ppermute | solution.py:329
  6.3 46.5 %collective-permute-start.7 = (bf16[2,24,2048]{2,1,0:T(8,128)(2,1)}, bf16[2,24,2048]{2,1,0:T(8,128)(2,1)S(1)}, u32[]{:S(2)}, u32[]{:S(2)}) collective-permute-start(bf16[2,24,2048]{2,1,0:T(8,128)(2,1)} %get-tuple-element.145), channel_id=1, source_target_pairs={{0,16},{8,24},{16,0},{24,8},{1,17},{9,25},{17,1},{25,9},{2,18},{10... | collective-permute-start | bytes 589832 | tf_op jit(solution)/shard_map/ppermute | solution.py:329
  8.9 44.0 %collective-permute-start.8 = (bf16[2,24,2048]{2,1,0:T(8,128)(2,1)}, bf16[2,24,2048]{2,1,0:T(8,128)(2,1)S(1)}, u32[]{:S(2)}, u32[]{:S(2)}) collective-permute-start(bf16[2,24,2048]{2,1,0:T(8,128)(2,1)} %get-tuple-element.146), channel_id=1, source_target_pairs={{0,24},{8,0},{16,8},{24,16},{1,25},{9,1},{17,9},{25,17},{2,26},{10... | collective-permute-start | bytes 589832 | tf_op jit(solution)/shard_map/ppermute | solution.py:329
  14.4 33.3 %all-to-all-start.1 = ((bf16[8,144,1024]{2,1,0:T(8,128)(2,1)}), bf16[8,144,1024]{2,1,0:T(8,128)(2,1)S(1)}, u32[]{:S(2)}, u32[]{:S(2)}) async-start(bf16[8,144,1024]{2,1,0:T(8,128)(2,1)} %turn_weights.3), calls=%async_computation.1 | async-start | bytes 4718592 | tf_op jit(solution)/shard_map/all_to_all | solution.py:346
  33.3 18.8 %copy-start.5 = (bf16[2,24,2048]{2,1,0:T(8,128)(2,1)S(1)}, bf16[2,24,2048]{2,1,0:T(8,128)(2,1)}, u32[]{:S(2)}) copy-start(bf16[2,24,2048]{2,1,0:T(8,128)(2,1)} %get-tuple-element.143) | copy-start | bytes 589828
  47.7 33.8 %all-to-all-start = ((bf16[8,144,1024]{2,1,0:T(8,128)(2,1)}), bf16[8,144,1024]{2,1,0:T(8,128)(2,1)}, u32[]{:S(2)}, u32[]{:S(2)}) async-start(bf16[8,144,1024]{2,1,0:T(8,128)(2,1)} %turn_weights.2), calls=%async_computation | async-start | bytes 4718592 | tf_op jit(solution)/shard_map/all_to_all | solution.py:346
  81.5 60.7 %collective-permute-start.12 = (bf16[96,2048]{1,0:T(8,128)(2,1)}, bf16[96,2048]{1,0:T(8,128)(2,1)}, u32[]{:S(2)}, u32[]{:S(2)}) collective-permute-start(bf16[96,2048]{1,0:T(8,128)(2,1)} %get-tuple-element.152.refs_0_), channel_id=1, source_target_pairs={{0,1},{1,0},{2,3},{3,2},{4,5},{5,4},{6,7},{7,6},{8,9},{9,8},{10,11... | collective-permute-start | bytes 1179656 | tf_op jit(solution)/shard_map/ppermute | solution.py:300
  81.5 62.3 %collective-permute-start.10 = (bf16[96,2048]{1,0:T(8,128)(2,1)}, bf16[96,2048]{1,0:T(8,128)(2,1)}, u32[]{:S(2)}, u32[]{:S(2)}) collective-permute-start(bf16[96,2048]{1,0:T(8,128)(2,1)} %get-tuple-element.152.refs_0_), channel_id=1, source_target_pairs={{0,4},{1,5},{2,6},{3,7},{4,0},{5,1},{6,2},{7,3},{8,12},{9,13},{10,... | collective-permute-start | bytes 1179656 | tf_op jit(solution)/shard_map/ppermute | solution.py:300
  82.1 62.0 %collective-permute-start.9 = (bf16[96,2048]{1,0:T(8,128)(2,1)}, bf16[96,2048]{1,0:T(8,128)(2,1)}, u32[]{:S(2)}, u32[]{:S(2)}) collective-permute-start(bf16[96,2048]{1,0:T(8,128)(2,1)} %get-tuple-element.152.refs_0_), channel_id=1, source_target_pairs={{0,2},{1,3},{2,0},{3,1},{4,6},{5,7},{6,4},{7,5},{8,10},{9,11},{10,... | collective-permute-start | bytes 1179656 | tf_op jit(solution)/shard_map/ppermute | solution.py:300
  89.9 17.4 %collective-permute-start.1 = (bf16[2,144,1024]{2,1,0:T(8,128)(2,1)}, bf16[2,144,1024]{2,1,0:T(8,128)(2,1)}, u32[]{:S(2)}, u32[]{:S(2)}) collective-permute-start(bf16[2,144,1024]{2,1,0:T(8,128)(2,1)} %pad_maximum_fusion.15), channel_id=1, source_target_pairs={{8,0},{16,8},{24,16},{9,1},{17,9},{25,17},{10,2},{18,10},{26,18},{... | collective-permute-start | bytes 1769480 | tf_op jit(solution)/shard_map/while/body/ppermute | solution.py:391
  92.1 17.3 %collective-permute-start = (bf16[2,144,1024]{2,1,0:T(8,128)(2,1)}, bf16[2,144,1024]{2,1,0:T(8,128)(2,1)}, u32[]{:S(2)}, u32[]{:S(2)}) collective-permute-start(bf16[2,144,1024]{2,1,0:T(8,128)(2,1)} %pad_maximum_fusion.14), channel_id=1, source_target_pairs={{0,8},{8,16},{16,24},{1,9},{9,17},{17,25},{2,10},{10,18},{18,26},{... | collective-permute-start | bytes 1769480 | tf_op jit(solution)/shard_map/while/body/ppermute | solution.py:391
  118.1 17.0 %collective-permute-start.1 = (bf16[2,144,1024]{2,1,0:T(8,128)(2,1)}, bf16[2,144,1024]{2,1,0:T(8,128)(2,1)}, u32[]{:S(2)}, u32[]{:S(2)}) collective-permute-start(bf16[2,144,1024]{2,1,0:T(8,128)(2,1)} %pad_maximum_fusion.15), channel_id=1, source_target_pairs={{8,0},{16,8},{24,16},{9,1},{17,9},{25,17},{10,2},{18,10},{26,18},{... | collective-permute-start | bytes 1769480 | tf_op jit(solution)/shard_map/while/body/ppermute | solution.py:391
  120.3 16.9 %collective-permute-start = (bf16[2,144,1024]{2,1,0:T(8,128)(2,1)}, bf16[2,144,1024]{2,1,0:T(8,128)(2,1)}, u32[]{:S(2)}, u32[]{:S(2)}) collective-permute-start(bf16[2,144,1024]{2,1,0:T(8,128)(2,1)} %pad_maximum_fusion.14), channel_id=1, source_target_pairs={{0,8},{8,16},{16,24},{1,9},{9,17},{17,25},{2,10},{10,18},{18,26},{... | collective-permute-start | bytes 1769480 | tf_op jit(solution)/shard_map/while/body/ppermute | solution.py:391
  140.8 12.2 %collective-permute-start.17 = (bf16[96,2048]{1,0:T(8,128)(2,1)}, bf16[96,2048]{1,0:T(8,128)(2,1)S(1)}, u32[]{:S(2)}, u32[]{:S(2)}) collective-permute-start(bf16[96,2048]{1,0:T(8,128)(2,1)} %get-tuple-element.153.refs_8_), channel_id=1, source_target_pairs={{0,4},{1,5},{2,6},{3,7},{4,0},{5,1},{6,2},{7,3},{8,12},{9,13},{10,... | collective-permute-start | bytes 1179656 | tf_op jit(solution)/shard_map/ppermute | solution.py:300
  142.2 12.3 %collective-permute-start.19 = (bf16[96,2048]{1,0:T(8,128)(2,1)}, bf16[96,2048]{1,0:T(8,128)(2,1)S(1)}, u32[]{:S(2)}, u32[]{:S(2)}) collective-permute-start(bf16[96,2048]{1,0:T(8,128)(2,1)} %get-tuple-element.153.refs_8_), channel_id=1, source_target_pairs={{0,1},{1,0},{2,3},{3,2},{4,5},{5,4},{6,7},{7,6},{8,9},{9,8},{10,11... | collective-permute-start | bytes 1179656 | tf_op jit(solution)/shard_map/ppermute | solution.py:300
  142.2 12.3 %collective-permute-start.16 = (bf16[96,2048]{1,0:T(8,128)(2,1)}, bf16[96,2048]{1,0:T(8,128)(2,1)S(1)}, u32[]{:S(2)}, u32[]{:S(2)}) collective-permute-start(bf16[96,2048]{1,0:T(8,128)(2,1)} %get-tuple-element.153.refs_8_), channel_id=1, source_target_pairs={{0,2},{1,3},{2,0},{3,1},{4,6},{5,7},{6,4},{7,5},{8,10},{9,11},{10,... | collective-permute-start | bytes 1179656 | tf_op jit(solution)/shard_map/ppermute | solution.py:300
  143.8 11.2 %collective-permute-start.14 = (bf16[96,2048]{1,0:T(8,128)(2,1)}, bf16[96,2048]{1,0:T(8,128)(2,1)S(1)}, u32[]{:S(2)}, u32[]{:S(2)}) collective-permute-start(bf16[96,2048]{1,0:T(8,128)(2,1)} %collective-permute-done.10.refs_2_), channel_id=1, source_target_pairs={{0,1},{1,0},{2,3},{3,2},{4,5},{5,4},{6,7},{7,6},{8,9},{9,8},{10,11... | collective-permute-start | bytes 1179656 | tf_op jit(solution)/shard_map/ppermute | solution.py:300
  144.0 14.5 %collective-permute-start.11 = (bf16[96,2048]{1,0:T(8,128)(2,1)}, bf16[96,2048]{1,0:T(8,128)(2,1)S(1)}, u32[]{:S(2)}, u32[]{:S(2)}) collective-permute-start(bf16[96,2048]{1,0:T(8,128)(2,1)} %collective-permute-done.9.refs_1_), channel_id=1, source_target_pairs={{0,4},{1,5},{2,6},{3,7},{4,0},{5,1},{6,2},{7,3},{8,12},{9,13},{10,... | collective-permute-start | bytes 1179656 | tf_op jit(solution)/shard_map/ppermute | solution.py:300
  153.1 12.0 %copy-start.8 = (bf16[96,2048]{1,0:T(8,128)(2,1)}, bf16[96,2048]{1,0:T(8,128)(2,1)S(1)}, u32[]{:S(2)}) copy-start(bf16[96,2048]{1,0:T(8,128)(2,1)S(1)} %collective-permute-done.17.refs_10_) | copy-start | bytes 1179652
  153.1 9.3 %collective-permute-start.18 = (bf16[96,2048]{1,0:T(8,128)(2,1)S(1)}, bf16[96,2048]{1,0:T(8,128)(2,1)S(1)}, u32[]{:S(2)}, u32[]{:S(2)}) collective-permute-start(bf16[96,2048]{1,0:T(8,128)(2,1)S(1)} %collective-permute-done.17.refs_10_), channel_id=1, source_target_pairs={{0,2},{1,3},{2,0},{3,1},{4,6},{5,7},{6,4},{7,5},{8,10},{9,11},{10,... | collective-permute-start | bytes 1179656 | tf_op jit(solution)/shard_map/ppermute | solution.py:300
  154.5 7.9 %copy-start.9 = (bf16[96,2048]{1,0:T(8,128)(2,1)}, bf16[96,2048]{1,0:T(8,128)(2,1)S(1)}, u32[]{:S(2)}) copy-start(bf16[96,2048]{1,0:T(8,128)(2,1)S(1)} %collective-permute-done.19.refs_12_) | copy-start | bytes 1179652
  154.5 8.6 %collective-permute-start.13 = (bf16[96,2048]{1,0:T(8,128)(2,1)}, bf16[96,2048]{1,0:T(8,128)(2,1)S(1)}, u32[]{:S(2)}, u32[]{:S(2)}) collective-permute-start(bf16[96,2048]{1,0:T(8,128)(2,1)} %collective-permute-done.9.refs_1_), channel_id=1, source_target_pairs={{0,1},{1,0},{2,3},{3,2},{4,5},{5,4},{6,7},{7,6},{8,9},{9,8},{10,11... | collective-permute-start | bytes 1179656 | tf_op jit(solution)/shard_map/ppermute | solution.py:300
  154.5 8.6 %copy-start.10 = (bf16[96,2048]{1,0:T(8,128)(2,1)}, bf16[96,2048]{1,0:T(8,128)(2,1)S(1)}, u32[]{:S(2)}) copy-start(bf16[96,2048]{1,0:T(8,128)(2,1)S(1)} %collective-permute-done.16.refs_9_) | copy-start | bytes 1179652
  154.5 8.5 %collective-permute-start.21 = (bf16[96,2048]{1,0:T(8,128)(2,1)S(1)}, bf16[96,2048]{1,0:T(8,128)(2,1)S(1)}, u32[]{:S(2)}, u32[]{:S(2)}) collective-permute-start(bf16[96,2048]{1,0:T(8,128)(2,1)S(1)} %collective-permute-done.17.refs_10_), channel_id=1, source_target_pairs={{0,1},{1,0},{2,3},{3,2},{4,5},{5,4},{6,7},{7,6},{8,9},{9,8},{10,11... | collective-permute-start | bytes 1179656 | tf_op jit(solution)/shard_map/ppermute | solution.py:300
  155.0 7.4 %copy-start.11 = (bf16[96,2048]{1,0:T(8,128)(2,1)}, bf16[96,2048]{1,0:T(8,128)(2,1)S(1)}, u32[]{:S(2)}) copy-start(bf16[96,2048]{1,0:T(8,128)(2,1)S(1)} %collective-permute-done.14.refs_6_) | copy-start | bytes 1179652
  155.0 8.1 %collective-permute-start.20 = (bf16[96,2048]{1,0:T(8,128)(2,1)S(1)}, bf16[96,2048]{1,0:T(8,128)(2,1)S(1)}, u32[]{:S(2)}, u32[]{:S(2)}) collective-permute-start(bf16[96,2048]{1,0:T(8,128)(2,1)S(1)} %collective-permute-done.16.refs_9_), channel_id=1, source_target_pairs={{0,1},{1,0},{2,3},{3,2},{4,5},{5,4},{6,7},{7,6},{8,9},{9,8},{10,11... | collective-permute-start | bytes 1179656 | tf_op jit(solution)/shard_map/ppermute | solution.py:300
  158.5 4.6 %collective-permute-start.15 = (bf16[96,2048]{1,0:T(8,128)(2,1)S(1)}, bf16[96,2048]{1,0:T(8,128)(2,1)S(1)}, u32[]{:S(2)}, u32[]{:S(2)}) collective-permute-start(bf16[96,2048]{1,0:T(8,128)(2,1)S(1)} %collective-permute-done.11.refs_3_), channel_id=1, source_target_pairs={{0,1},{1,0},{2,3},{3,2},{4,5},{5,4},{6,7},{7,6},{8,9},{9,8},{10,11... | collective-permute-start | bytes 1179656 | tf_op jit(solution)/shard_map/ppermute | solution.py:300
  162.4 1.7 collective-permute-start.22
  197.0 20.3 %all-to-all-start.2 = ((f32[8,288,128]{2,1,0:T(8,128)}), f32[8,288,128]{2,1,0:T(8,128)S(1)}, u32[]{:S(2)}, u32[]{:S(2)}) async-start(f32[8,288,128]{2,1,0:T(8,128)} %get-tuple-element.154), calls=%async_computation.2 | async-start | bytes 2359296 | tf_op jit(solution)/shard_map/all_to_all | solution.py:408
  223.6 7.7 %collective-permute-start.29 = (bf16[80,1152]{1,0:T(8,128)(2,1)}, bf16[80,1152]{1,0:T(8,128)(2,1)S(1)}, u32[]{:S(2)}, u32[]{:S(2)}) collective-permute-start(bf16[80,1152]{1,0:T(8,128)(2,1)} %get-tuple-element.167.refs_0_), channel_id=1, source_target_pairs={{0,8},{8,16},{16,24},{24,0},{1,9},{9,17},{17,25},{25,1},{2,10},{10... | collective-permute-start | bytes 552968 | tf_op jit(solution)/shard_map/ppermute | solution.py:431
  224.9 11.1 %collective-permute-start.32 = (bf16[80,1152]{1,0:T(8,128)(2,1)}, bf16[80,1152]{1,0:T(8,128)(2,1)S(1)}, u32[]{:S(2)}, u32[]{:S(2)}) collective-permute-start(bf16[80,1152]{1,0:T(8,128)(2,1)} %get-tuple-element.168.refs_4_), channel_id=1, source_target_pairs={{0,24},{8,0},{16,8},{24,16},{1,25},{9,1},{17,9},{25,17},{2,26},{10... | collective-permute-start | bytes 552968 | tf_op jit(solution)/shard_map/ppermute | solution.py:432
  231.2 20.1 %copy-start.27 = (bf16[80,1152]{1,0:T(8,128)(2,1)}, bf16[80,1152]{1,0:T(8,128)(2,1)S(1)}, u32[]{:S(2)}) copy-start(bf16[80,1152]{1,0:T(8,128)(2,1)S(1)} %collective-permute-done.29.refs_1_) | copy-start | bytes 552964
  231.2 7.8 %collective-permute-start.30 = (bf16[80,1152]{1,0:T(8,128)(2,1)S(1)}, bf16[80,1152]{1,0:T(8,128)(2,1)S(1)}, u32[]{:S(2)}, u32[]{:S(2)}) collective-permute-start(bf16[80,1152]{1,0:T(8,128)(2,1)S(1)} %collective-permute-done.29.refs_1_), channel_id=1, source_target_pairs={{0,8},{8,16},{16,24},{24,0},{1,9},{9,17},{17,25},{25,1},{2,10},{10... | collective-permute-start | bytes 552968 | tf_op jit(solution)/shard_map/ppermute | solution.py:431
  235.9 15.3 %copy-start.28 = (bf16[80,1152]{1,0:T(8,128)(2,1)}, bf16[80,1152]{1,0:T(8,128)(2,1)S(1)}, u32[]{:S(2)}) copy-start(bf16[80,1152]{1,0:T(8,128)(2,1)S(1)} %collective-permute-done.32.refs_5_) | copy-start | bytes 552964
  235.9 9.8 %collective-permute-start.33 = (bf16[80,1152]{1,0:T(8,128)(2,1)S(1)}, bf16[80,1152]{1,0:T(8,128)(2,1)S(1)}, u32[]{:S(2)}, u32[]{:S(2)}) collective-permute-start(bf16[80,1152]{1,0:T(8,128)(2,1)S(1)} %collective-permute-done.32.refs_5_), channel_id=1, source_target_pairs={{0,24},{8,0},{16,8},{24,16},{1,25},{9,1},{17,9},{25,17},{2,26},{10... | collective-permute-start | bytes 552968 | tf_op jit(solution)/shard_map/ppermute | solution.py:432
  239.0 12.3 %copy-start.29 = (bf16[80,1152]{1,0:T(8,128)(2,1)}, bf16[80,1152]{1,0:T(8,128)(2,1)S(1)}, u32[]{:S(2)}) copy-start(bf16[80,1152]{1,0:T(8,128)(2,1)S(1)} %collective-permute-done.30.refs_2_) | copy-start | bytes 552964
  239.0 8.6 %collective-permute-start.31 = (bf16[80,1152]{1,0:T(8,128)(2,1)S(1)}, bf16[80,1152]{1,0:T(8,128)(2,1)S(1)}, u32[]{:S(2)}, u32[]{:S(2)}) collective-permute-start(bf16[80,1152]{1,0:T(8,128)(2,1)S(1)} %collective-permute-done.30.refs_2_), channel_id=1, source_target_pairs={{0,8},{8,16},{16,24},{24,0},{1,9},{9,17},{17,25},{25,1},{2,10},{10... | collective-permute-start | bytes 552968 | tf_op jit(solution)/shard_map/ppermute | solution.py:431
  245.7 5.6 %copy-start.30 = (bf16[80,1152]{1,0:T(8,128)(2,1)}, bf16[80,1152]{1,0:T(8,128)(2,1)S(1)}, u32[]{:S(2)}) copy-start(bf16[80,1152]{1,0:T(8,128)(2,1)S(1)} %collective-permute-done.33.refs_6_) | copy-start | bytes 552964
  245.8 5.5 %collective-permute-start.34 = (bf16[80,1152]{1,0:T(8,128)(2,1)S(1)}, bf16[80,1152]{1,0:T(8,128)(2,1)S(1)}, u32[]{:S(2)}, u32[]{:S(2)}) collective-permute-start(bf16[80,1152]{1,0:T(8,128)(2,1)S(1)} %collective-permute-done.33.refs_6_), channel_id=1, source_target_pairs={{0,24},{8,0},{16,8},{24,16},{1,25},{9,1},{17,9},{25,17},{2,26},{10... | collective-permute-start | bytes 552968 | tf_op jit(solution)/shard_map/ppermute | solution.py:432
  255.1 5.9 %copy-start.20 = (bf16[128,1152]{1,0:T(8,128)(2,1)S(1)}, bf16[128,1152]{1,0:T(8,128)(2,1)}, u32[]{:S(2)}) copy-start(bf16[128,1152]{1,0:T(8,128)(2,1)} %get-tuple-element.166.refs_4_) | copy-start | bytes 884740
  255.1 53.8 %all-to-all-start.5 = ((bf16[8,80,1152]{2,1,0:T(8,128)(2,1)}), bf16[8,80,1152]{2,1,0:T(8,128)(2,1)S(1)}, u32[]{:S(2)}, u32[]{:S(2)}) async-start(bf16[8,80,1152]{2,1,0:T(8,128)(2,1)} %choose_pieces.4), calls=%async_computation.5 | async-start | bytes 2949120 | tf_op jit(solution)/shard_map/all_to_all | solution.py:435
  260.2 11.8 %collective-permute-start.23 = (bf16[128,1152]{1,0:T(8,128)(2,1)S(1)}, bf16[128,1152]{1,0:T(8,128)(2,1)S(1)}, u32[]{:S(2)}, u32[]{:S(2)}) collective-permute-start(bf16[128,1152]{1,0:T(8,128)(2,1)S(1)} %copy-done.19), channel_id=1, source_target_pairs={{0,8},{8,16},{16,24},{24,0},{1,9},{9,17},{17,25},{25,1},{2,10},{10... | collective-permute-start | bytes 884744 | tf_op jit(solution)/shard_map/ppermute | solution.py:431
  261.0 15.6 %collective-permute-start.26 = (bf16[128,1152]{1,0:T(8,128)(2,1)S(1)}, bf16[128,1152]{1,0:T(8,128)(2,1)S(1)}, u32[]{:S(2)}, u32[]{:S(2)}) collective-permute-start(bf16[128,1152]{1,0:T(8,128)(2,1)S(1)} %copy-done.20), channel_id=1, source_target_pairs={{0,24},{8,0},{16,8},{24,16},{1,25},{9,1},{17,9},{25,17},{2,26},{10... | collective-permute-start | bytes 884744 | tf_op jit(solution)/shard_map/ppermute | solution.py:432
  272.0 32.5 %copy-start.21 = (bf16[128,1152]{1,0:T(8,128)(2,1)}, bf16[128,1152]{1,0:T(8,128)(2,1)S(1)}, u32[]{:S(2)}) copy-start(bf16[128,1152]{1,0:T(8,128)(2,1)S(1)} %collective-permute-done.23.refs_1_) | copy-start | bytes 884740
  272.0 14.5 %collective-permute-start.24 = (bf16[128,1152]{1,0:T(8,128)(2,1)S(1)}, bf16[128,1152]{1,0:T(8,128)(2,1)S(1)}, u32[]{:S(2)}, u32[]{:S(2)}) collective-permute-start(bf16[128,1152]{1,0:T(8,128)(2,1)S(1)} %collective-permute-done.23.refs_1_), channel_id=1, source_target_pairs={{0,8},{8,16},{16,24},{24,0},{1,9},{9,17},{17,25},{25,1},{2,10},{10... | collective-permute-start | bytes 884744 | tf_op jit(solution)/shard_map/ppermute | solution.py:431
  276.6 27.9 %copy-start.22 = (bf16[128,1152]{1,0:T(8,128)(2,1)}, bf16[128,1152]{1,0:T(8,128)(2,1)S(1)}, u32[]{:S(2)}) copy-start(bf16[128,1152]{1,0:T(8,128)(2,1)S(1)} %collective-permute-done.26.refs_5_) | copy-start | bytes 884740
  276.6 16.2 %collective-permute-start.27 = (bf16[128,1152]{1,0:T(8,128)(2,1)S(1)}, bf16[128,1152]{1,0:T(8,128)(2,1)S(1)}, u32[]{:S(2)}, u32[]{:S(2)}) collective-permute-start(bf16[128,1152]{1,0:T(8,128)(2,1)S(1)} %collective-permute-done.26.refs_5_), channel_id=1, source_target_pairs={{0,24},{8,0},{16,8},{24,16},{1,25},{9,1},{17,9},{25,17},{2,26},{10... | collective-permute-start | bytes 884744 | tf_op jit(solution)/shard_map/ppermute | solution.py:432
  286.4 18.1 %copy-start.23 = (bf16[128,1152]{1,0:T(8,128)(2,1)}, bf16[128,1152]{1,0:T(8,128)(2,1)S(1)}, u32[]{:S(2)}) copy-start(bf16[128,1152]{1,0:T(8,128)(2,1)S(1)} %collective-permute-done.24.refs_2_) | copy-start | bytes 884740
  286.5 13.7 %collective-permute-start.25 = (bf16[128,1152]{1,0:T(8,128)(2,1)S(1)}, bf16[128,1152]{1,0:T(8,128)(2,1)S(1)}, u32[]{:S(2)}, u32[]{:S(2)}) collective-permute-start(bf16[128,1152]{1,0:T(8,128)(2,1)S(1)} %collective-permute-done.24.refs_2_), channel_id=1, source_target_pairs={{0,8},{8,16},{16,24},{24,0},{1,9},{9,17},{17,25},{25,1},{2,10},{10... | collective-permute-start | bytes 884744 | tf_op jit(solution)/shard_map/ppermute | solution.py:431
  292.8 11.8 %copy-start.24 = (bf16[128,1152]{1,0:T(8,128)(2,1)}, bf16[128,1152]{1,0:T(8,128)(2,1)S(1)}, u32[]{:S(2)}) copy-start(bf16[128,1152]{1,0:T(8,128)(2,1)S(1)} %collective-permute-done.27.refs_6_) | copy-start | bytes 884740
  292.8 11.8 %collective-permute-start.28 = (bf16[128,1152]{1,0:T(8,128)(2,1)S(1)}, bf16[128,1152]{1,0:T(8,128)(2,1)S(1)}, u32[]{:S(2)}, u32[]{:S(2)}) collective-permute-start(bf16[128,1152]{1,0:T(8,128)(2,1)S(1)} %collective-permute-done.27.refs_6_), channel_id=1, source_target_pairs={{0,24},{8,0},{16,8},{24,16},{1,25},{9,1},{17,9},{25,17},{2,26},{10... | collective-permute-start | bytes 884744 | tf_op jit(solution)/shard_map/ppermute | solution.py:432
  308.9 5.4 %copy-start.34 = (bf16[48,1152]{1,0:T(8,128)(2,1)S(1)}, bf16[48,1152]{1,0:T(8,128)(2,1)}, u32[]{:S(2)}) copy-start(bf16[48,1152]{1,0:T(8,128)(2,1)} %get-tuple-element.170.refs_4_) | copy-start | bytes 331780
  310.1 33.0 %all-to-all-start.4 = ((bf16[8,128,1152]{2,1,0:T(8,128)(2,1)}), bf16[8,128,1152]{2,1,0:T(8,128)(2,1)S(1)}, u32[]{:S(2)}, u32[]{:S(2)}) async-start(bf16[8,128,1152]{2,1,0:T(8,128)(2,1)} %choose_pieces.3), calls=%async_computation.4 | async-start | bytes 4718592 | tf_op jit(solution)/shard_map/all_to_all | solution.py:435
  313.7 7.8 %collective-permute-start.35 = (bf16[48,1152]{1,0:T(8,128)(2,1)S(1)}, bf16[48,1152]{1,0:T(8,128)(2,1)S(1)}, u32[]{:S(2)}, u32[]{:S(2)}) collective-permute-start(bf16[48,1152]{1,0:T(8,128)(2,1)S(1)} %copy-done.33), channel_id=1, source_target_pairs={{0,8},{8,16},{16,24},{24,0},{1,9},{9,17},{17,25},{25,1},{2,10},{10... | collective-permute-start | bytes 331784 | tf_op jit(solution)/shard_map/ppermute | solution.py:431
  314.3 8.1 %collective-permute-start.38 = (bf16[48,1152]{1,0:T(8,128)(2,1)S(1)}, bf16[48,1152]{1,0:T(8,128)(2,1)S(1)}, u32[]{:S(2)}, u32[]{:S(2)}) collective-permute-start(bf16[48,1152]{1,0:T(8,128)(2,1)S(1)} %copy-done.34), channel_id=1, source_target_pairs={{0,24},{8,0},{16,8},{24,16},{1,25},{9,1},{17,9},{25,17},{2,26},{10... | collective-permute-start | bytes 331784 | tf_op jit(solution)/shard_map/ppermute | solution.py:432
  321.5 14.6 %copy-start.35 = (bf16[48,1152]{1,0:T(8,128)(2,1)}, bf16[48,1152]{1,0:T(8,128)(2,1)S(1)}, u32[]{:S(2)}) copy-start(bf16[48,1152]{1,0:T(8,128)(2,1)S(1)} %collective-permute-done.35.refs_1_) | copy-start | bytes 331780
  321.5 6.9 %collective-permute-start.36 = (bf16[48,1152]{1,0:T(8,128)(2,1)S(1)}, bf16[48,1152]{1,0:T(8,128)(2,1)S(1)}, u32[]{:S(2)}, u32[]{:S(2)}) collective-permute-start(bf16[48,1152]{1,0:T(8,128)(2,1)S(1)} %collective-permute-done.35.refs_1_), channel_id=1, source_target_pairs={{0,8},{8,16},{16,24},{24,0},{1,9},{9,17},{17,25},{25,1},{2,10},{10... | collective-permute-start | bytes 331784 | tf_op jit(solution)/shard_map/ppermute | solution.py:431
  322.4 13.7 %copy-start.36 = (bf16[48,1152]{1,0:T(8,128)(2,1)}, bf16[48,1152]{1,0:T(8,128)(2,1)S(1)}, u32[]{:S(2)}) copy-start(bf16[48,1152]{1,0:T(8,128)(2,1)S(1)} %collective-permute-done.38.refs_5_) | copy-start | bytes 331780
  322.4 7.5 %collective-permute-start.39 = (bf16[48,1152]{1,0:T(8,128)(2,1)S(1)}, bf16[48,1152]{1,0:T(8,128)(2,1)S(1)}, u32[]{:S(2)}, u32[]{:S(2)}) collective-permute-start(bf16[48,1152]{1,0:T(8,128)(2,1)S(1)} %collective-permute-done.38.refs_5_), channel_id=1, source_target_pairs={{0,24},{8,0},{16,8},{24,16},{1,25},{9,1},{17,9},{25,17},{2,26},{10... | collective-permute-start | bytes 331784 | tf_op jit(solution)/shard_map/ppermute | solution.py:432
  328.4 7.7 %copy-start.37 = (bf16[48,1152]{1,0:T(8,128)(2,1)}, bf16[48,1152]{1,0:T(8,128)(2,1)S(1)}, u32[]{:S(2)}) copy-start(bf16[48,1152]{1,0:T(8,128)(2,1)S(1)} %collective-permute-done.36.refs_2_) | copy-start | bytes 331780
  328.4 6.6 %collective-permute-start.37 = (bf16[48,1152]{1,0:T(8,128)(2,1)S(1)}, bf16[48,1152]{1,0:T(8,128)(2,1)S(1)}, u32[]{:S(2)}, u32[]{:S(2)}) collective-permute-start(bf16[48,1152]{1,0:T(8,128)(2,1)S(1)} %collective-permute-done.36.refs_2_), channel_id=1, source_target_pairs={{0,8},{8,16},{16,24},{24,0},{1,9},{9,17},{17,25},{25,1},{2,10},{10... | collective-permute-start | bytes 331784 | tf_op jit(solution)/shard_map/ppermute | solution.py:431
  329.9 6.2 %copy-start.38 = (bf16[48,1152]{1,0:T(8,128)(2,1)}, bf16[48,1152]{1,0:T(8,128)(2,1)S(1)}, u32[]{:S(2)}) copy-start(bf16[48,1152]{1,0:T(8,128)(2,1)S(1)} %collective-permute-done.39.refs_6_) | copy-start | bytes 331780
  329.9 6.2 %collective-permute-start.40 = (bf16[48,1152]{1,0:T(8,128)(2,1)S(1)}, bf16[48,1152]{1,0:T(8,128)(2,1)S(1)}, u32[]{:S(2)}, u32[]{:S(2)}) collective-permute-start(bf16[48,1152]{1,0:T(8,128)(2,1)S(1)} %collective-permute-done.39.refs_6_), channel_id=1, source_target_pairs={{0,24},{8,0},{16,8},{24,16},{1,25},{9,1},{17,9},{25,17},{2,26},{10... | collective-permute-start | bytes 331784 | tf_op jit(solution)/shard_map/ppermute | solution.py:432
  343.0 19.1 %all-to-all-start.6 = ((bf16[8,48,1152]{2,1,0:T(8,128)(2,1)}), bf16[8,48,1152]{2,1,0:T(8,128)(2,1)S(1)}, u32[]{:S(2)}, u32[]{:S(2)}) async-start(bf16[8,48,1152]{2,1,0:T(8,128)(2,1)} %choose_pieces.5), calls=%async_computation.6 | async-start | bytes 1769472 | tf_op jit(solution)/shard_map/all_to_all | solution.py:435
  (22 other events, 53.0 us)
where the time goes:
time: 364 us; the launch traced here: 363 us
  waiting for transfers between devices  155 us (43%)
  starting transfers between devices  86.9 us (24%)
  Pallas kernels  42.1 us (12%)
  local copies, waits for them, and re-layouts  35.3 us (10%)
  blocking collectives  21 us (6%)
  other arithmetic  11.1 us (3%)
  loops' own time  11.1 us (3%)
    all_to_all x2, waiting for transfers between devices, step_body(): lax.all_to_all(turned, 'dp', split_axis=0, concat_axis=0, tiled=True)  42.1 us
    ppermute x9, waiting for transfers between devices, step_body(): rings[0].append(lax.ppermute(rings[0][-1], 'expert', forward))  36 us
    ppermute x4, waiting for transfers between devices, trip(): got = lax.ppermute(sent, 'expert', pairs)  22.9 us
    ppermute x9, waiting for transfers between devices, step_body(): rings[1].append(lax.ppermute(rings[1][-1], 'expert', backward))  22.1 us
    all_to_all x1, blocking collectives, step_body(): lax.all_to_all(partial[chunk], 'dp', split_axis=0, concat_axis=0, tiled=T...  21 us
    unnamed x92, local copies, waits for them, and re-layouts  20.6 us
    ppermute x9, starting transfers between devices, step_body(): rings[1].append(lax.ppermute(rings[1][-1], 'expert', backward))  20.5 us
    ppermute x14, waiting for transfers between devices, swap(): return lax.ppermute(value, 'dp', [(i, i ^ mask) for i in range(count)])  16.7 us
  transfers between devices with their start and end apart: 45, of which 28 were waited for; matrix products, arithmetic and copies ran while one was open for 11% of the time, Pallas kernels for 6%

commit v1 on v0

--- a/solution.py
+++ b/solution.py
@@ -269,6 +269,25 @@
     )(arrived, master, moment, second, *held)
 
 
+def join_kernel(halves_ref, out_ref):
+    for half in range(2):
+        out_ref[:, half, :] = halves_ref[half]
+
+
+def join_halves(halves):
+    _, rows, columns = halves.shape
+    block = min(64, rows)
+    return pl.pallas_call(
+        join_kernel,
+        grid=(rows // block,),
+        out_shape=jax.ShapeDtypeStruct((rows, 2, columns), halves.dtype),
+        in_specs=[pl.BlockSpec((2, block, columns), lambda i: (0, i, 0))],
+        out_specs=pl.BlockSpec((block, 2, columns), lambda i: (i, 0, 0)),
+        cost_estimate=pl.CostEstimate(flops=2_000_000_000, bytes_accessed=5_000_000, transcendentals=0),
+        name="join_halves",
+    )(halves)
+
+
 def choose_kernel(count, want_ref, *refs):
     sources = refs[:count]
     out_ref = refs[count]
@@ -421,8 +440,7 @@
     backward = [(i, (i - 1) % planes) for i in range(planes)]
     outs = []
     for kind in range(3):
-        out = jnp.transpose(updated[kind], (1, 0, 2))[None]
-        outs.append(out)
+        outs.append(join_halves(updated[kind])[None])
     replica = None
     begin = 0
     for own_halves in fresh:

time: 364 us -> 364 us (level)
  Pallas kernels: 42.1 us -> 54.2 us
  local copies, waits for them, and re-layouts: 35.3 us -> 23.7 us
  waiting for transfers between devices: 155 us -> 151 us
    pallas_call x0 -> x3, Pallas kernels: none -> 12.1 us  [join_halves(): pl.pallas_call(join_kernel, grid=(rows // block,), out_shape=jax.ShapeDty...]
    unnamed x92 -> x85, local copies, waits for them, and re-layouts: 20.6 us -> 9.02 us
  transfers between devices with their start and end apart: 45 -> 45, of which waited for: 28 -> 27; matrix products, arithmetic and copies ran while one was open for 11% -> 8% of each run, Pallas kernels for 6% -> 9%
where the time goes in v1:
time: 364 us; the launch traced here: 363 us
  waiting for transfers between devices  151 us (41%)
  starting transfers between devices  89.7 us (25%)
  Pallas kernels  54.2 us (15%)
  local copies, waits for them, and re-layouts  23.7 us (7%)
  blocking collectives  21 us (6%)
  loops' own time  11.2 us (3%)
  other arithmetic  11.1 us (3%)
    all_to_all x2, waiting for transfers between devices, step_body(): lax.all_to_all(turned, 'dp', split_axis=0, concat_axis=0, tiled=True)  42.1 us
    ppermute x9, waiting for transfers between devices, step_body(): rings[0].append(lax.ppermute(rings[0][-1], 'expert', forward))  32.6 us
    ppermute x4, waiting for transfers between devices, trip(): got = lax.ppermute(sent, 'expert', pairs)  22.9 us
    ppermute x9, waiting for transfers between devices, step_body(): rings[1].append(lax.ppermute(rings[1][-1], 'expert', backward))  21.7 us
    all_to_all x1, blocking collectives, step_body(): lax.all_to_all(partial[chunk], 'dp', split_axis=0, concat_axis=0, tiled=T...  21 us
    ppermute x9, starting transfers between devices, step_body(): rings[1].append(lax.ppermute(rings[1][-1], 'expert', backward))  20.8 us
    ppermute x9, starting transfers between devices, step_body(): rings[0].append(lax.ppermute(rings[0][-1], 'expert', forward))  17.1 us
    ppermute x14, waiting for transfers between devices, swap(): return lax.ppermute(value, 'dp', [(i, i ^ mask) for i in range(count)])  16.7 us
  transfers between devices with their start and end apart: 45, of which 27 were waited for; matrix products, arithmetic and copies ran while one was open for 8% of the time, Pallas kernels for 9%

profile of v1, /device:TPU:0, one launch (start us, length us, event | category | flops | bytes accessed | tf_op | source)
XLA Modules:
  0.0 362.7 jit_solution(10167580191204064555)
XLA Ops:
  0.6 2.6 keep_rows.1
  3.2 3.0 collective-permute-start.6
  6.3 2.6 collective-permute-start.7
  10.2 4.2 %turn_weights.3 = bf16[8,144,1024]{2,1,0:T(8,128)(2,1)} custom-call(bf16[2048,1152]{1,0:T(8,128)(2,1)} %bitcast.92), custom_call_target="tpu_custom_call" | custom-call | flops 4000000000 | bytes 5000000 | tf_op jit(solution)/shard_map/turn_weights/pallas_call | solution.py:99
  14.4 3.9 %all-to-all-start.1 = ((bf16[8,144,1024]{2,1,0:T(8,128)(2,1)}), bf16[8,144,1024]{2,1,0:T(8,128)(2,1)S(1)}, u32[]{:S(2)}, u32[]{:S(2)}) async-start(bf16[8,144,1024]{2,1,0:T(8,128)(2,1)} %turn_weights.3), calls=%async_computation.1 | async-start | bytes 4718592 | tf_op jit(solution)/shard_map/all_to_all | solution.py:365
  20.8 3.2 copy.60
  24.3 4.2 %turn_weights.2 = bf16[8,144,1024]{2,1,0:T(8,128)(2,1)} custom-call(bf16[2048,1152]{1,0:T(8,128)(2,1)} %bitcast.93), custom_call_target="tpu_custom_call" | custom-call | flops 4000000000 | bytes 5000000 | tf_op jit(solution)/shard_map/turn_weights/pallas_call | solution.py:99
  28.5 4.8 %copy_bitcast_fusion = (f32[2,256,1152]{2,1,0:T(8,128)}, f32[2,256,1152]{2,1,0:T(8,128)}) fusion(f32[1,256,2,1152]{3,2,1,0:T(2,128)} %param.26, f32[1,256,2,1152]{3,2,1,0:T(2,128)} %param.25), kind=kLoop, calls=%fused_computation.35 | loop fusion | bytes 9437184 | tf_op jit(solution)/shard_map/transpose | solution.py:372
  33.4 14.4 %all-to-all-done.1.own1_ref = bf16[8,144,1024]{2,1,0:T(8,128)(2,1)S(1)} async-done(((bf16[8,144,1024]{2,1,0:T(8,128)(2,1)}), bf16[8,144,1024]{2,1,0:T(8,128)(2,1)S(1)}, u32[]{:S(2)}, u32[]{:S(2)}) %all-to-all-start.1) | async-done | bytes 2359328 | tf_op jit(solution)/shard_map/all_to_all | solution.py:365
  47.7 4.4 %all-to-all-start = ((bf16[8,144,1024]{2,1,0:T(8,128)(2,1)}), bf16[8,144,1024]{2,1,0:T(8,128)(2,1)}, u32[]{:S(2)}, u32[]{:S(2)}) async-start(bf16[8,144,1024]{2,1,0:T(8,128)(2,1)} %turn_weights.2), calls=%async_computation | async-start | bytes 4718592 | tf_op jit(solution)/shard_map/all_to_all | solution.py:365
  53.8 27.7 %all-to-all-done.own0_ref = bf16[8,144,1024]{2,1,0:T(8,128)(2,1)} async-done(((bf16[8,144,1024]{2,1,0:T(8,128)(2,1)}), bf16[8,144,1024]{2,1,0:T(8,128)(2,1)}, u32[]{:S(2)}, u32[]{:S(2)}) %all-to-all-start) | async-done | bytes 2359328 | tf_op jit(solution)/shard_map/all_to_all | solution.py:365
  82.8 56.8 %while.30 = (s32[]{:T(128)}, bf16[2,2,144,1024]{3,2,1,0:T(8,128)(2,1)S(1)}, s32[]{:T(128)}, pred[2,3,2,2]{3,2,1,0:T(4,128)(4,1)S(1)}, s32[2,3,2]{1,2,0:T(2,128)S...) while((s32[]{:T(128)}, ...), condition=%wide.region_9.10_spmd, body=%wide.region_8.9_spmd.sunk | while | flops 1769483 | bytes 12976463 | solution.py:415
  92.1 5.4 %collective-permute-start = (bf16[2,144,1024]{2,1,0:T(8,128)(2,1)}, bf16[2,144,1024]{2,1,0:T(8,128)(2,1)}, u32[]{:S(2)}, u32[]{:S(2)}) collective-permute-start(bf16[2,144,1024]{2,1,0:T(8,128)(2,1)} %pad_maximum_fusion.14), channel_id=1, source_target_pairs={{0,8},{8,16},{16,24},{1,9},{9,17},{17,25},{2,10},{10,18},{18,26},{... | collective-permute-start | bytes 1769480 | tf_op jit(solution)/shard_map/while/body/ppermute | solution.py:410
  97.5 9.8 %collective-permute-done.1 = bf16[2,144,1024]{2,1,0:T(8,128)(2,1)} collective-permute-done((bf16[2,144,1024]{2,1,0:T(8,128)(2,1)}, bf16[2,144,1024]{2,1,0:T(8,128)(2,1)}, u32[]{:S(2)}, u32[]{:S(2)}) %collective-permute-start.1) | collective-permute-done | bytes 589856 | tf_op jit(solution)/shard_map/while/body/ppermute | solution.py:410
  107.4 2.0 collective-permute-done
  109.4 1.7 select_select_fusion.6
  120.4 5.9 %collective-permute-start = (bf16[2,144,1024]{2,1,0:T(8,128)(2,1)}, bf16[2,144,1024]{2,1,0:T(8,128)(2,1)}, u32[]{:S(2)}, u32[]{:S(2)}) collective-permute-start(bf16[2,144,1024]{2,1,0:T(8,128)(2,1)} %pad_maximum_fusion.14), channel_id=1, source_target_pairs={{0,8},{8,16},{16,24},{1,9},{9,17},{17,25},{2,10},{10,18},{18,26},{... | collective-permute-start | bytes 1769480 | tf_op jit(solution)/shard_map/while/body/ppermute | solution.py:410
  126.3 9.0 %collective-permute-done.1 = bf16[2,144,1024]{2,1,0:T(8,128)(2,1)} collective-permute-done((bf16[2,144,1024]{2,1,0:T(8,128)(2,1)}, bf16[2,144,1024]{2,1,0:T(8,128)(2,1)}, u32[]{:S(2)}, u32[]{:S(2)}) %collective-permute-start.1) | collective-permute-done | bytes 589856 | tf_op jit(solution)/shard_map/while/body/ppermute | solution.py:410
  135.2 2.0 collective-permute-done
  137.3 1.7 select_select_fusion.6
  142.4 1.6 collective-permute-start.16
  144.8 8.5 %collective-permute-done.17.refs_10_ = bf16[96,2048]{1,0:T(8,128)(2,1)S(1)} collective-permute-done((bf16[96,2048]{1,0:T(8,128)(2,1)}, bf16[96,2048]{1,0:T(8,128)(2,1)S(1)}, u32[]{:S(2)}, u32[]{:S(2)}) %collective-permute-start.17) | collective-permute-done | bytes 393248 | tf_op jit(solution)/shard_map/ppermute | solution.py:319
  153.2 1.5 collective-permute-start.18
  155.3 3.4 collective-permute-done.11.refs_3_
  158.7 3.9 %collective-permute-done.18.refs_11_ = bf16[96,2048]{1,0:T(8,128)(2,1)S(1)} collective-permute-done((bf16[96,2048]{1,0:T(8,128)(2,1)S(1)}, bf16[96,2048]{1,0:T(8,128)(2,1)S(1)}, u32[]{:S(2)}, u32[]{:S(2)}) %collective-permute-start.18) | collective-permute-done | bytes 393248 | tf_op jit(solution)/shard_map/ppermute | solution.py:319
  165.2 10.9 %half_grads.1 = (f32[8,288,128]{2,1,0:T(8,128)}, f32[8,288,128]{2,1,0:T(8,128)}) custom-call(s32[2,2]{1,0:T(2,128)} %pad_add_fusion.3.table_ref, bf16[8,144,1024]{2,1,0:T(8,128)(2,1)} %all-to-all-done.own0_ref, bf16[8,144,1024]{2,1,0:T(8,128)(2,1)S(1)} %get-tuple-element.617, bf16[2,2,144,1024]{3,2,1,0:T(8,128)(2,1)S(1)} %get-tuple-element.151.far_ref, ...), custom_call_target="tpu_custom_call" | custom-call | flops 10000000000 | bytes 10000000 | tf_op jit(solution)/shard_map/half_grads/pallas_call | solution.py:204
  176.1 21.0 %all_to_all.35.arrived_ref = f32[8,288,128]{2,1,0:T(8,128)} all-to-all(f32[8,288,128]{2,1,0:T(8,128)} %get-tuple-element.158), channel_id=1, replica_groups=mesh['expert'=4,'dp'=8] {'dp'}, dimensions={0} | all-to-all | bytes 2359296 | tf_op jit(solution)/shard_map/all_to_all | solution.py:427
  197.1 3.6 all-to-all-start.2
  200.7 5.3 %update_rows.2 = (f32[2,256,1152]{2,1,0:T(8,128)}, f32[2,256,1152]{2,1,0:T(8,128)}, f32[2,256,1152]{2,1,0:T(8,128)}, bf16[128,1152]{1,0:T(8,128)(2,1)}, bf16[128,1152]{1,0:T(8,128)(2,1)}) custom-call(f32[8,288,128]{2,1,0:T(8,128)} %all_to_all.35.arrived_ref, f32[2,256,1152]{2,1,0:T(8,128)} %bitcast.87, f32[2,256,1152]{2,1,0:T(8,128)} %get-tuple-element.156.moment_ref, ...), custom_call_target="tpu_custom_call" | custom-call | flops 4000000000 | bytes 9000000 | tf_op jit(solution)/shard_map/update_rows/pallas_call | solution.py:257
  206.0 11.4 %all-to-all-done.2.arrived_ref = f32[8,288,128]{2,1,0:T(8,128)S(1)} async-done(((f32[8,288,128]{2,1,0:T(8,128)}), f32[8,288,128]{2,1,0:T(8,128)S(1)}, u32[]{:S(2)}, u32[]{:S(2)}) %all-to-all-start.2) | async-done | bytes 1179680 | tf_op jit(solution)/shard_map/all_to_all | solution.py:427
  218.4 5.3 %update_rows.3 = (f32[2,256,1152]{2,1,0:T(8,128)}, f32[2,256,1152]{2,1,0:T(8,128)}, f32[2,256,1152]{2,1,0:T(8,128)}, bf16[80,1152]{1,0:T(8,128)(2,1)}, bf16[80,1...) custom-call(f32[8,288,128]{2,1,0:T(8,128)} %copy-done.2, ...), custom_call_target="tpu_custom_call", output_to_operand_aliasing={{0}: (4, {}), {1}: (5, {}), {2}: (6, {})} | custom-call | flops 4000000000 | bytes 9000000 | tf_op jit(solution)/shard_map/update_rows/pallas_call | solution.py:257
  225.0 2.5 collective-permute-start.32
  227.5 3.8 %collective-permute-done.29.refs_1_ = bf16[80,1152]{1,0:T(8,128)(2,1)S(1)} collective-permute-done((bf16[80,1152]{1,0:T(8,128)(2,1)}, bf16[80,1152]{1,0:T(8,128)(2,1)S(1)}, u32[]{:S(2)}, u32[]{:S(2)}) %collective-permute-start.29) | collective-permute-done | bytes 184352 | tf_op jit(solution)/shard_map/ppermute | solution.py:449
  232.1 4.0 %collective-permute-done.32.refs_5_ = bf16[80,1152]{1,0:T(8,128)(2,1)S(1)} collective-permute-done((bf16[80,1152]{1,0:T(8,128)(2,1)}, bf16[80,1152]{1,0:T(8,128)(2,1)S(1)}, u32[]{:S(2)}, u32[]{:S(2)}) %collective-permute-start.32) | collective-permute-done | bytes 184352 | tf_op jit(solution)/shard_map/ppermute | solution.py:450
  236.1 1.8 collective-permute-start.33
  239.2 6.9 %collective-permute-done.33.refs_6_ = bf16[80,1152]{1,0:T(8,128)(2,1)S(1)} collective-permute-done((bf16[80,1152]{1,0:T(8,128)(2,1)S(1)}, bf16[80,1152]{1,0:T(8,128)(2,1)S(1)}, u32[]{:S(2)}, u32[]{:S(2)}) %collective-permute-start.33) | collective-permute-done | bytes 184352 | tf_op jit(solution)/shard_map/ppermute | solution.py:450
  247.8 3.8 %collective-permute-done.34.refs_7_ = bf16[80,1152]{1,0:T(8,128)(2,1)S(1)} collective-permute-done((bf16[80,1152]{1,0:T(8,128)(2,1)S(1)}, bf16[80,1152]{1,0:T(8,128)(2,1)S(1)}, u32[]{:S(2)}, u32[]{:S(2)}) %collective-permute-start.34) | collective-permute-done | bytes 184352 | tf_op jit(solution)/shard_map/ppermute | solution.py:450
  252.3 3.1 choose_pieces.4
  255.4 4.9 %all-to-all-start.5 = ((bf16[8,80,1152]{2,1,0:T(8,128)(2,1)}), bf16[8,80,1152]{2,1,0:T(8,128)(2,1)S(1)}, u32[]{:S(2)}, u32[]{:S(2)}) async-start(bf16[8,80,1152]{2,1,0:T(8,128)(2,1)} %choose_pieces.4), calls=%async_computation.5 | async-start | bytes 2949120 | tf_op jit(solution)/shard_map/all_to_all | solution.py:453
  261.1 3.1 collective-permute-start.26
  264.2 7.9 %collective-permute-done.23.refs_1_ = bf16[128,1152]{1,0:T(8,128)(2,1)S(1)} collective-permute-done((bf16[128,1152]{1,0:T(8,128)(2,1)S(1)}, bf16[128,1152]{1,0:T(8,128)(2,1)S(1)}, u32[]{:S(2)}, u32[]{:S(2)}) %collective-permute-start.23) | collective-permute-done | bytes 294944 | tf_op jit(solution)/shard_map/ppermute | solution.py:449
  272.1 4.2 %collective-permute-start.24 = (bf16[128,1152]{1,0:T(8,128)(2,1)S(1)}, bf16[128,1152]{1,0:T(8,128)(2,1)S(1)}, u32[]{:S(2)}, u32[]{:S(2)}) collective-permute-start(bf16[128,1152]{1,0:T(8,128)(2,1)S(1)} %collective-permute-done.23.refs_1_), channel_id=1, source_target_pairs={{0,8},{8,16},{16,24},{24,0},{1,9},{9,17},{17,25},{25,1},{2,10},{10... | collective-permute-start | bytes 884744 | tf_op jit(solution)/shard_map/ppermute | solution.py:449
  276.7 2.5 collective-permute-start.27
  279.2 5.6 %collective-permute-done.24.refs_2_ = bf16[128,1152]{1,0:T(8,128)(2,1)S(1)} collective-permute-done((bf16[128,1152]{1,0:T(8,128)(2,1)S(1)}, bf16[128,1152]{1,0:T(8,128)(2,1)S(1)}, u32[]{:S(2)}, u32[]{:S(2)}) %collective-permute-start.24) | collective-permute-done | bytes 294944 | tf_op jit(solution)/shard_map/ppermute | solution.py:449
  284.8 6.8 %collective-permute-start.25 = (bf16[128,1152]{1,0:T(8,128)(2,1)S(1)}, bf16[128,1152]{1,0:T(8,128)(2,1)S(1)}, u32[]{:S(2)}, u32[]{:S(2)}) collective-permute-start(bf16[128,1152]{1,0:T(8,128)(2,1)S(1)} %collective-permute-done.24.refs_2_), channel_id=1, source_target_pairs={{0,8},{8,16},{16,24},{24,0},{1,9},{9,17},{17,25},{25,1},{2,10},{10... | collective-permute-start | bytes 884744 | tf_op jit(solution)/shard_map/ppermute | solution.py:449
  291.5 2.2 collective-permute-start.28
  293.7 4.5 %collective-permute-done.25.refs_3_ = bf16[128,1152]{1,0:T(8,128)(2,1)S(1)} collective-permute-done((bf16[128,1152]{1,0:T(8,128)(2,1)S(1)}, bf16[128,1152]{1,0:T(8,128)(2,1)S(1)}, u32[]{:S(2)}, u32[]{:S(2)}) %collective-permute-start.25) | collective-permute-done | bytes 294944 | tf_op jit(solution)/shard_map/ppermute | solution.py:449
  298.3 5.0 %collective-permute-done.28.refs_7_ = bf16[128,1152]{1,0:T(8,128)(2,1)S(1)} collective-permute-done((bf16[128,1152]{1,0:T(8,128)(2,1)S(1)}, bf16[128,1152]{1,0:T(8,128)(2,1)S(1)}, u32[]{:S(2)}, u32[]{:S(2)}) %collective-permute-start.28) | collective-permute-done | bytes 294944 | tf_op jit(solution)/shard_map/ppermute | solution.py:450
  304.0 3.6 %choose_pieces.3 = bf16[8,128,1152]{2,1,0:T(8,128)(2,1)} custom-call(s32[8]{0:T(128)} %fusion.9.want_ref, bf16[128,1152]{1,0:T(8,128)(2,1)} %get-tuple-element.165.refs_0_, bf16[128,1152]{1,0:T(8,128)(2,1)} %copy-done.19, bf16[128,1152]{1,0:T(8,128)(2,1)} %copy-done.21, bf16[128,1152]{1,0:T(8,128)(2,1)} %copy-done.23, ...), custom_call_target="tpu_custom_call" | custom-call | flops 1500000000 | bytes 4000000 | tf_op jit(solution)/shard_map/choose_pieces/pallas_call | solution.py:307
  308.7 3.8 %all-to-all-start.4 = ((bf16[8,128,1152]{2,1,0:T(8,128)(2,1)}), bf16[8,128,1152]{2,1,0:T(8,128)(2,1)S(1)}, u32[]{:S(2)}, u32[]{:S(2)}) async-start(bf16[8,128,1152]{2,1,0:T(8,128)(2,1)} %choose_pieces.3), calls=%async_computation.4 | async-start | bytes 4718592 | tf_op jit(solution)/shard_map/all_to_all | solution.py:453
  313.4 3.1 collective-permute-start.38
  316.4 3.9 %collective-permute-done.35.refs_1_ = bf16[48,1152]{1,0:T(8,128)(2,1)S(1)} collective-permute-done((bf16[48,1152]{1,0:T(8,128)(2,1)S(1)}, bf16[48,1152]{1,0:T(8,128)(2,1)S(1)}, u32[]{:S(2)}, u32[]{:S(2)}) %collective-permute-start.35) | collective-permute-done | bytes 110624 | tf_op jit(solution)/shard_map/ppermute | solution.py:449
  321.6 2.6 collective-permute-start.39
  324.2 3.3 collective-permute-done.36.refs_2_
  327.5 1.8 collective-permute-start.37
  329.3 2.5 collective-permute-start.40
  331.8 2.3 collective-permute-done.37.refs_3_
  335.9 2.7 choose_pieces.5
  338.6 3.4 all-to-all-done.4
  342.0 3.6 all-to-all-start.6
  345.5 4.1 %join_halves.3 = f32[256,2,1152]{2,1,0:T(2,128)} custom-call(f32[2,256,1152]{2,1,0:T(8,128)} %get-tuple-element.162.halves_ref), custom_call_target="tpu_custom_call" | custom-call | flops 2000000000 | bytes 5000000 | tf_op jit(solution)/shard_map/join_halves/pallas_call | solution.py:280
  349.6 4.0 %join_halves.4 = f32[256,2,1152]{2,1,0:T(2,128)} custom-call(f32[2,256,1152]{2,1,0:T(8,128)} %get-tuple-element.163.halves_ref), custom_call_target="tpu_custom_call" | custom-call | flops 2000000000 | bytes 5000000 | tf_op jit(solution)/shard_map/join_halves/pallas_call | solution.py:280
  353.6 4.0 %join_halves.5 = f32[256,2,1152]{2,1,0:T(2,128)} custom-call(f32[2,256,1152]{2,1,0:T(8,128)} %get-tuple-element.164.halves_ref), custom_call_target="tpu_custom_call" | custom-call | flops 2000000000 | bytes 5000000 | tf_op jit(solution)/shard_map/join_halves/pallas_call | solution.py:280
  357.7 2.8 dynamic_update_slice.9
  (180 shorter events, 38.7 us)
Async XLA Ops:
  3.2 49.6 %collective-permute-start.6 = (bf16[2,24,2048]{2,1,0:T(8,128)(2,1)}, bf16[2,24,2048]{2,1,0:T(8,128)(2,1)S(1)}, u32[]{:S(2)}, u32[]{:S(2)}) collective-permute-start(bf16[2,24,2048]{2,1,0:T(8,128)(2,1)} %get-tuple-element.144), channel_id=1, source_target_pairs={{0,8},{8,16},{16,24},{24,0},{1,9},{9,17},{17,25},{25,1},{2,10},{10... | collective-permute-start | bytes 589832 | tf_op jit(solution)/shard_map/ppermute | solution.py:348
  6.3 46.5 %collective-permute-start.7 = (bf16[2,24,2048]{2,1,0:T(8,128)(2,1)}, bf16[2,24,2048]{2,1,0:T(8,128)(2,1)S(1)}, u32[]{:S(2)}, u32[]{:S(2)}) collective-permute-start(bf16[2,24,2048]{2,1,0:T(8,128)(2,1)} %get-tuple-element.145), channel_id=1, source_target_pairs={{0,16},{8,24},{16,0},{24,8},{1,17},{9,25},{17,1},{25,9},{2,18},{10... | collective-permute-start | bytes 589832 | tf_op jit(solution)/shard_map/ppermute | solution.py:348
  8.9 44.0 %collective-permute-start.8 = (bf16[2,24,2048]{2,1,0:T(8,128)(2,1)}, bf16[2,24,2048]{2,1,0:T(8,128)(2,1)S(1)}, u32[]{:S(2)}, u32[]{:S(2)}) collective-permute-start(bf16[2,24,2048]{2,1,0:T(8,128)(2,1)} %get-tuple-element.146), channel_id=1, source_target_pairs={{0,24},{8,0},{16,8},{24,16},{1,25},{9,1},{17,9},{25,17},{2,26},{10... | collective-permute-start | bytes 589832 | tf_op jit(solution)/shard_map/ppermute | solution.py:348
  14.4 33.3 %all-to-all-start.1 = ((bf16[8,144,1024]{2,1,0:T(8,128)(2,1)}), bf16[8,144,1024]{2,1,0:T(8,128)(2,1)S(1)}, u32[]{:S(2)}, u32[]{:S(2)}) async-start(bf16[8,144,1024]{2,1,0:T(8,128)(2,1)} %turn_weights.3), calls=%async_computation.1 | async-start | bytes 4718592 | tf_op jit(solution)/shard_map/all_to_all | solution.py:365
  33.3 18.8 %copy-start.3 = (bf16[2,24,2048]{2,1,0:T(8,128)(2,1)S(1)}, bf16[2,24,2048]{2,1,0:T(8,128)(2,1)}, u32[]{:S(2)}) copy-start(bf16[2,24,2048]{2,1,0:T(8,128)(2,1)} %get-tuple-element.143) | copy-start | bytes 589828
  47.7 33.8 %all-to-all-start = ((bf16[8,144,1024]{2,1,0:T(8,128)(2,1)}), bf16[8,144,1024]{2,1,0:T(8,128)(2,1)}, u32[]{:S(2)}, u32[]{:S(2)}) async-start(bf16[8,144,1024]{2,1,0:T(8,128)(2,1)} %turn_weights.2), calls=%async_computation | async-start | bytes 4718592 | tf_op jit(solution)/shard_map/all_to_all | solution.py:365
  81.5 60.9 %collective-permute-start.12 = (bf16[96,2048]{1,0:T(8,128)(2,1)}, bf16[96,2048]{1,0:T(8,128)(2,1)}, u32[]{:S(2)}, u32[]{:S(2)}) collective-permute-start(bf16[96,2048]{1,0:T(8,128)(2,1)} %get-tuple-element.152.refs_0_), channel_id=1, source_target_pairs={{0,1},{1,0},{2,3},{3,2},{4,5},{5,4},{6,7},{7,6},{8,9},{9,8},{10,11... | collective-permute-start | bytes 1179656 | tf_op jit(solution)/shard_map/ppermute | solution.py:319
  81.5 62.5 %collective-permute-start.10 = (bf16[96,2048]{1,0:T(8,128)(2,1)}, bf16[96,2048]{1,0:T(8,128)(2,1)}, u32[]{:S(2)}, u32[]{:S(2)}) collective-permute-start(bf16[96,2048]{1,0:T(8,128)(2,1)} %get-tuple-element.152.refs_0_), channel_id=1, source_target_pairs={{0,4},{1,5},{2,6},{3,7},{4,0},{5,1},{6,2},{7,3},{8,12},{9,13},{10,... | collective-permute-start | bytes 1179656 | tf_op jit(solution)/shard_map/ppermute | solution.py:319
  82.1 62.1 %collective-permute-start.9 = (bf16[96,2048]{1,0:T(8,128)(2,1)}, bf16[96,2048]{1,0:T(8,128)(2,1)}, u32[]{:S(2)}, u32[]{:S(2)}) collective-permute-start(bf16[96,2048]{1,0:T(8,128)(2,1)} %get-tuple-element.152.refs_0_), channel_id=1, source_target_pairs={{0,2},{1,3},{2,0},{3,1},{4,6},{5,7},{6,4},{7,5},{8,10},{9,11},{10,... | collective-permute-start | bytes 1179656 | tf_op jit(solution)/shard_map/ppermute | solution.py:319
  90.0 17.4 %collective-permute-start.1 = (bf16[2,144,1024]{2,1,0:T(8,128)(2,1)}, bf16[2,144,1024]{2,1,0:T(8,128)(2,1)}, u32[]{:S(2)}, u32[]{:S(2)}) collective-permute-start(bf16[2,144,1024]{2,1,0:T(8,128)(2,1)} %pad_maximum_fusion.15), channel_id=1, source_target_pairs={{8,0},{16,8},{24,16},{9,1},{17,9},{25,17},{10,2},{18,10},{26,18},{... | collective-permute-start | bytes 1769480 | tf_op jit(solution)/shard_map/while/body/ppermute | solution.py:410
  92.1 17.3 %collective-permute-start = (bf16[2,144,1024]{2,1,0:T(8,128)(2,1)}, bf16[2,144,1024]{2,1,0:T(8,128)(2,1)}, u32[]{:S(2)}, u32[]{:S(2)}) collective-permute-start(bf16[2,144,1024]{2,1,0:T(8,128)(2,1)} %pad_maximum_fusion.14), channel_id=1, source_target_pairs={{0,8},{8,16},{16,24},{1,9},{9,17},{17,25},{2,10},{10,18},{18,26},{... | collective-permute-start | bytes 1769480 | tf_op jit(solution)/shard_map/while/body/ppermute | solution.py:410
  118.2 17.0 %collective-permute-start.1 = (bf16[2,144,1024]{2,1,0:T(8,128)(2,1)}, bf16[2,144,1024]{2,1,0:T(8,128)(2,1)}, u32[]{:S(2)}, u32[]{:S(2)}) collective-permute-start(bf16[2,144,1024]{2,1,0:T(8,128)(2,1)} %pad_maximum_fusion.15), channel_id=1, source_target_pairs={{8,0},{16,8},{24,16},{9,1},{17,9},{25,17},{10,2},{18,10},{26,18},{... | collective-permute-start | bytes 1769480 | tf_op jit(solution)/shard_map/while/body/ppermute | solution.py:410
  120.4 16.9 %collective-permute-start = (bf16[2,144,1024]{2,1,0:T(8,128)(2,1)}, bf16[2,144,1024]{2,1,0:T(8,128)(2,1)}, u32[]{:S(2)}, u32[]{:S(2)}) collective-permute-start(bf16[2,144,1024]{2,1,0:T(8,128)(2,1)} %pad_maximum_fusion.14), channel_id=1, source_target_pairs={{0,8},{8,16},{16,24},{1,9},{9,17},{17,25},{2,10},{10,18},{18,26},{... | collective-permute-start | bytes 1769480 | tf_op jit(solution)/shard_map/while/body/ppermute | solution.py:410
  141.0 12.2 %collective-permute-start.17 = (bf16[96,2048]{1,0:T(8,128)(2,1)}, bf16[96,2048]{1,0:T(8,128)(2,1)S(1)}, u32[]{:S(2)}, u32[]{:S(2)}) collective-permute-start(bf16[96,2048]{1,0:T(8,128)(2,1)} %get-tuple-element.153.refs_8_), channel_id=1, source_target_pairs={{0,4},{1,5},{2,6},{3,7},{4,0},{5,1},{6,2},{7,3},{8,12},{9,13},{10,... | collective-permute-start | bytes 1179656 | tf_op jit(solution)/shard_map/ppermute | solution.py:319
  142.4 12.3 %collective-permute-start.19 = (bf16[96,2048]{1,0:T(8,128)(2,1)}, bf16[96,2048]{1,0:T(8,128)(2,1)S(1)}, u32[]{:S(2)}, u32[]{:S(2)}) collective-permute-start(bf16[96,2048]{1,0:T(8,128)(2,1)} %get-tuple-element.153.refs_8_), channel_id=1, source_target_pairs={{0,1},{1,0},{2,3},{3,2},{4,5},{5,4},{6,7},{7,6},{8,9},{9,8},{10,11... | collective-permute-start | bytes 1179656 | tf_op jit(solution)/shard_map/ppermute | solution.py:319
  142.4 12.3 %collective-permute-start.16 = (bf16[96,2048]{1,0:T(8,128)(2,1)}, bf16[96,2048]{1,0:T(8,128)(2,1)S(1)}, u32[]{:S(2)}, u32[]{:S(2)}) collective-permute-start(bf16[96,2048]{1,0:T(8,128)(2,1)} %get-tuple-element.153.refs_8_), channel_id=1, source_target_pairs={{0,2},{1,3},{2,0},{3,1},{4,6},{5,7},{6,4},{7,5},{8,10},{9,11},{10,... | collective-permute-start | bytes 1179656 | tf_op jit(solution)/shard_map/ppermute | solution.py:319
  144.0 11.2 %collective-permute-start.14 = (bf16[96,2048]{1,0:T(8,128)(2,1)}, bf16[96,2048]{1,0:T(8,128)(2,1)S(1)}, u32[]{:S(2)}, u32[]{:S(2)}) collective-permute-start(bf16[96,2048]{1,0:T(8,128)(2,1)} %collective-permute-done.10.refs_2_), channel_id=1, source_target_pairs={{0,1},{1,0},{2,3},{3,2},{4,5},{5,4},{6,7},{7,6},{8,9},{9,8},{10,11... | collective-permute-start | bytes 1179656 | tf_op jit(solution)/shard_map/ppermute | solution.py:319
  144.2 14.5 %collective-permute-start.11 = (bf16[96,2048]{1,0:T(8,128)(2,1)}, bf16[96,2048]{1,0:T(8,128)(2,1)S(1)}, u32[]{:S(2)}, u32[]{:S(2)}) collective-permute-start(bf16[96,2048]{1,0:T(8,128)(2,1)} %collective-permute-done.9.refs_1_), channel_id=1, source_target_pairs={{0,4},{1,5},{2,6},{3,7},{4,0},{5,1},{6,2},{7,3},{8,12},{9,13},{10,... | collective-permute-start | bytes 1179656 | tf_op jit(solution)/shard_map/ppermute | solution.py:319
  153.2 12.0 %copy-start.6 = (bf16[96,2048]{1,0:T(8,128)(2,1)}, bf16[96,2048]{1,0:T(8,128)(2,1)S(1)}, u32[]{:S(2)}) copy-start(bf16[96,2048]{1,0:T(8,128)(2,1)S(1)} %collective-permute-done.17.refs_10_) | copy-start | bytes 1179652
  153.2 9.3 %collective-permute-start.18 = (bf16[96,2048]{1,0:T(8,128)(2,1)S(1)}, bf16[96,2048]{1,0:T(8,128)(2,1)S(1)}, u32[]{:S(2)}, u32[]{:S(2)}) collective-permute-start(bf16[96,2048]{1,0:T(8,128)(2,1)S(1)} %collective-permute-done.17.refs_10_), channel_id=1, source_target_pairs={{0,2},{1,3},{2,0},{3,1},{4,6},{5,7},{6,4},{7,5},{8,10},{9,11},{10,... | collective-permute-start | bytes 1179656 | tf_op jit(solution)/shard_map/ppermute | solution.py:319
  154.7 7.9 %copy-start.7 = (bf16[96,2048]{1,0:T(8,128)(2,1)}, bf16[96,2048]{1,0:T(8,128)(2,1)S(1)}, u32[]{:S(2)}) copy-start(bf16[96,2048]{1,0:T(8,128)(2,1)S(1)} %collective-permute-done.19.refs_12_) | copy-start | bytes 1179652
  154.7 8.6 %collective-permute-start.13 = (bf16[96,2048]{1,0:T(8,128)(2,1)}, bf16[96,2048]{1,0:T(8,128)(2,1)S(1)}, u32[]{:S(2)}, u32[]{:S(2)}) collective-permute-start(bf16[96,2048]{1,0:T(8,128)(2,1)} %collective-permute-done.9.refs_1_), channel_id=1, source_target_pairs={{0,1},{1,0},{2,3},{3,2},{4,5},{5,4},{6,7},{7,6},{8,9},{9,8},{10,11... | collective-permute-start | bytes 1179656 | tf_op jit(solution)/shard_map/ppermute | solution.py:319
  154.7 8.6 %copy-start.8 = (bf16[96,2048]{1,0:T(8,128)(2,1)}, bf16[96,2048]{1,0:T(8,128)(2,1)S(1)}, u32[]{:S(2)}) copy-start(bf16[96,2048]{1,0:T(8,128)(2,1)S(1)} %collective-permute-done.16.refs_9_) | copy-start | bytes 1179652
  154.7 8.6 %collective-permute-start.21 = (bf16[96,2048]{1,0:T(8,128)(2,1)S(1)}, bf16[96,2048]{1,0:T(8,128)(2,1)S(1)}, u32[]{:S(2)}, u32[]{:S(2)}) collective-permute-start(bf16[96,2048]{1,0:T(8,128)(2,1)S(1)} %collective-permute-done.17.refs_10_), channel_id=1, source_target_pairs={{0,1},{1,0},{2,3},{3,2},{4,5},{5,4},{6,7},{7,6},{8,9},{9,8},{10,11... | collective-permute-start | bytes 1179656 | tf_op jit(solution)/shard_map/ppermute | solution.py:319
  155.2 7.4 %copy-start.9 = (bf16[96,2048]{1,0:T(8,128)(2,1)}, bf16[96,2048]{1,0:T(8,128)(2,1)S(1)}, u32[]{:S(2)}) copy-start(bf16[96,2048]{1,0:T(8,128)(2,1)S(1)} %collective-permute-done.14.refs_6_) | copy-start | bytes 1179652
  155.2 8.1 %collective-permute-start.20 = (bf16[96,2048]{1,0:T(8,128)(2,1)S(1)}, bf16[96,2048]{1,0:T(8,128)(2,1)S(1)}, u32[]{:S(2)}, u32[]{:S(2)}) collective-permute-start(bf16[96,2048]{1,0:T(8,128)(2,1)S(1)} %collective-permute-done.16.refs_9_), channel_id=1, source_target_pairs={{0,1},{1,0},{2,3},{3,2},{4,5},{5,4},{6,7},{7,6},{8,9},{9,8},{10,11... | collective-permute-start | bytes 1179656 | tf_op jit(solution)/shard_map/ppermute | solution.py:319
  158.7 4.6 %collective-permute-start.15 = (bf16[96,2048]{1,0:T(8,128)(2,1)S(1)}, bf16[96,2048]{1,0:T(8,128)(2,1)S(1)}, u32[]{:S(2)}, u32[]{:S(2)}) collective-permute-start(bf16[96,2048]{1,0:T(8,128)(2,1)S(1)} %collective-permute-done.11.refs_3_), channel_id=1, source_target_pairs={{0,1},{1,0},{2,3},{3,2},{4,5},{5,4},{6,7},{7,6},{8,9},{9,8},{10,11... | collective-permute-start | bytes 1179656 | tf_op jit(solution)/shard_map/ppermute | solution.py:319
  162.6 1.7 collective-permute-start.22
  197.1 20.3 %all-to-all-start.2 = ((f32[8,288,128]{2,1,0:T(8,128)}), f32[8,288,128]{2,1,0:T(8,128)S(1)}, u32[]{:S(2)}, u32[]{:S(2)}) async-start(f32[8,288,128]{2,1,0:T(8,128)} %get-tuple-element.154), calls=%async_computation.2 | async-start | bytes 2359296 | tf_op jit(solution)/shard_map/all_to_all | solution.py:427
  223.7 7.7 %collective-permute-start.29 = (bf16[80,1152]{1,0:T(8,128)(2,1)}, bf16[80,1152]{1,0:T(8,128)(2,1)S(1)}, u32[]{:S(2)}, u32[]{:S(2)}) collective-permute-start(bf16[80,1152]{1,0:T(8,128)(2,1)} %get-tuple-element.167.refs_0_), channel_id=1, source_target_pairs={{0,8},{8,16},{16,24},{24,0},{1,9},{9,17},{17,25},{25,1},{2,10},{10... | collective-permute-start | bytes 552968 | tf_op jit(solution)/shard_map/ppermute | solution.py:449
  225.0 11.1 %collective-permute-start.32 = (bf16[80,1152]{1,0:T(8,128)(2,1)}, bf16[80,1152]{1,0:T(8,128)(2,1)S(1)}, u32[]{:S(2)}, u32[]{:S(2)}) collective-permute-start(bf16[80,1152]{1,0:T(8,128)(2,1)} %get-tuple-element.168.refs_4_), channel_id=1, source_target_pairs={{0,24},{8,0},{16,8},{24,16},{1,25},{9,1},{17,9},{25,17},{2,26},{10... | collective-permute-start | bytes 552968 | tf_op jit(solution)/shard_map/ppermute | solution.py:450
  231.4 20.2 %copy-start.25 = (bf16[80,1152]{1,0:T(8,128)(2,1)}, bf16[80,1152]{1,0:T(8,128)(2,1)S(1)}, u32[]{:S(2)}) copy-start(bf16[80,1152]{1,0:T(8,128)(2,1)S(1)} %collective-permute-done.29.refs_1_) | copy-start | bytes 552964
  231.4 7.8 %collective-permute-start.30 = (bf16[80,1152]{1,0:T(8,128)(2,1)S(1)}, bf16[80,1152]{1,0:T(8,128)(2,1)S(1)}, u32[]{:S(2)}, u32[]{:S(2)}) collective-permute-start(bf16[80,1152]{1,0:T(8,128)(2,1)S(1)} %collective-permute-done.29.refs_1_), channel_id=1, source_target_pairs={{0,8},{8,16},{16,24},{24,0},{1,9},{9,17},{17,25},{25,1},{2,10},{10... | collective-permute-start | bytes 552968 | tf_op jit(solution)/shard_map/ppermute | solution.py:449
  236.1 15.5 %copy-start.26 = (bf16[80,1152]{1,0:T(8,128)(2,1)}, bf16[80,1152]{1,0:T(8,128)(2,1)S(1)}, u32[]{:S(2)}) copy-start(bf16[80,1152]{1,0:T(8,128)(2,1)S(1)} %collective-permute-done.32.refs_5_) | copy-start | bytes 552964
  236.1 10.0 %collective-permute-start.33 = (bf16[80,1152]{1,0:T(8,128)(2,1)S(1)}, bf16[80,1152]{1,0:T(8,128)(2,1)S(1)}, u32[]{:S(2)}, u32[]{:S(2)}) collective-permute-start(bf16[80,1152]{1,0:T(8,128)(2,1)S(1)} %collective-permute-done.32.refs_5_), channel_id=1, source_target_pairs={{0,24},{8,0},{16,8},{24,16},{1,25},{9,1},{17,9},{25,17},{2,26},{10... | collective-permute-start | bytes 552968 | tf_op jit(solution)/shard_map/ppermute | solution.py:450
  239.2 12.4 %copy-start.27 = (bf16[80,1152]{1,0:T(8,128)(2,1)}, bf16[80,1152]{1,0:T(8,128)(2,1)S(1)}, u32[]{:S(2)}) copy-start(bf16[80,1152]{1,0:T(8,128)(2,1)S(1)} %collective-permute-done.30.refs_2_) | copy-start | bytes 552964
  239.2 8.6 %collective-permute-start.31 = (bf16[80,1152]{1,0:T(8,128)(2,1)S(1)}, bf16[80,1152]{1,0:T(8,128)(2,1)S(1)}, u32[]{:S(2)}, u32[]{:S(2)}) collective-permute-start(bf16[80,1152]{1,0:T(8,128)(2,1)S(1)} %collective-permute-done.30.refs_2_), channel_id=1, source_target_pairs={{0,8},{8,16},{16,24},{24,0},{1,9},{9,17},{17,25},{25,1},{2,10},{10... | collective-permute-start | bytes 552968 | tf_op jit(solution)/shard_map/ppermute | solution.py:449
  246.1 5.6 %copy-start.28 = (bf16[80,1152]{1,0:T(8,128)(2,1)}, bf16[80,1152]{1,0:T(8,128)(2,1)S(1)}, u32[]{:S(2)}) copy-start(bf16[80,1152]{1,0:T(8,128)(2,1)S(1)} %collective-permute-done.33.refs_6_) | copy-start | bytes 552964
  246.1 5.5 %collective-permute-start.34 = (bf16[80,1152]{1,0:T(8,128)(2,1)S(1)}, bf16[80,1152]{1,0:T(8,128)(2,1)S(1)}, u32[]{:S(2)}, u32[]{:S(2)}) collective-permute-start(bf16[80,1152]{1,0:T(8,128)(2,1)S(1)} %collective-permute-done.33.refs_6_), channel_id=1, source_target_pairs={{0,24},{8,0},{16,8},{24,16},{1,25},{9,1},{17,9},{25,17},{2,26},{10... | collective-permute-start | bytes 552968 | tf_op jit(solution)/shard_map/ppermute | solution.py:450
  255.4 5.7 %copy-start.18 = (bf16[128,1152]{1,0:T(8,128)(2,1)S(1)}, bf16[128,1152]{1,0:T(8,128)(2,1)}, u32[]{:S(2)}) copy-start(bf16[128,1152]{1,0:T(8,128)(2,1)} %get-tuple-element.166.refs_4_) | copy-start | bytes 884740
  255.4 52.2 %all-to-all-start.5 = ((bf16[8,80,1152]{2,1,0:T(8,128)(2,1)}), bf16[8,80,1152]{2,1,0:T(8,128)(2,1)S(1)}, u32[]{:S(2)}, u32[]{:S(2)}) async-start(bf16[8,80,1152]{2,1,0:T(8,128)(2,1)} %choose_pieces.4), calls=%async_computation.5 | async-start | bytes 2949120 | tf_op jit(solution)/shard_map/all_to_all | solution.py:453
  260.3 11.8 %collective-permute-start.23 = (bf16[128,1152]{1,0:T(8,128)(2,1)S(1)}, bf16[128,1152]{1,0:T(8,128)(2,1)S(1)}, u32[]{:S(2)}, u32[]{:S(2)}) collective-permute-start(bf16[128,1152]{1,0:T(8,128)(2,1)S(1)} %copy-done.17), channel_id=1, source_target_pairs={{0,8},{8,16},{16,24},{24,0},{1,9},{9,17},{17,25},{25,1},{2,10},{10... | collective-permute-start | bytes 884744 | tf_op jit(solution)/shard_map/ppermute | solution.py:449
  261.1 15.6 %collective-permute-start.26 = (bf16[128,1152]{1,0:T(8,128)(2,1)S(1)}, bf16[128,1152]{1,0:T(8,128)(2,1)S(1)}, u32[]{:S(2)}, u32[]{:S(2)}) collective-permute-start(bf16[128,1152]{1,0:T(8,128)(2,1)S(1)} %copy-done.18), channel_id=1, source_target_pairs={{0,24},{8,0},{16,8},{24,16},{1,25},{9,1},{17,9},{25,17},{2,26},{10... | collective-permute-start | bytes 884744 | tf_op jit(solution)/shard_map/ppermute | solution.py:450
  272.1 31.1 %copy-start.19 = (bf16[128,1152]{1,0:T(8,128)(2,1)}, bf16[128,1152]{1,0:T(8,128)(2,1)S(1)}, u32[]{:S(2)}) copy-start(bf16[128,1152]{1,0:T(8,128)(2,1)S(1)} %collective-permute-done.23.refs_1_) | copy-start | bytes 884740
  272.1 12.7 %collective-permute-start.24 = (bf16[128,1152]{1,0:T(8,128)(2,1)S(1)}, bf16[128,1152]{1,0:T(8,128)(2,1)S(1)}, u32[]{:S(2)}, u32[]{:S(2)}) collective-permute-start(bf16[128,1152]{1,0:T(8,128)(2,1)S(1)} %collective-permute-done.23.refs_1_), channel_id=1, source_target_pairs={{0,8},{8,16},{16,24},{24,0},{1,9},{9,17},{17,25},{25,1},{2,10},{10... | collective-permute-start | bytes 884744 | tf_op jit(solution)/shard_map/ppermute | solution.py:449
  276.7 26.5 %copy-start.20 = (bf16[128,1152]{1,0:T(8,128)(2,1)}, bf16[128,1152]{1,0:T(8,128)(2,1)S(1)}, u32[]{:S(2)}) copy-start(bf16[128,1152]{1,0:T(8,128)(2,1)S(1)} %collective-permute-done.26.refs_5_) | copy-start | bytes 884740
  276.7 14.8 %collective-permute-start.27 = (bf16[128,1152]{1,0:T(8,128)(2,1)S(1)}, bf16[128,1152]{1,0:T(8,128)(2,1)S(1)}, u32[]{:S(2)}, u32[]{:S(2)}) collective-permute-start(bf16[128,1152]{1,0:T(8,128)(2,1)S(1)} %collective-permute-done.26.refs_5_), channel_id=1, source_target_pairs={{0,24},{8,0},{16,8},{24,16},{1,25},{9,1},{17,9},{25,17},{2,26},{10... | collective-permute-start | bytes 884744 | tf_op jit(solution)/shard_map/ppermute | solution.py:450
  284.8 18.5 %copy-start.21 = (bf16[128,1152]{1,0:T(8,128)(2,1)}, bf16[128,1152]{1,0:T(8,128)(2,1)S(1)}, u32[]{:S(2)}) copy-start(bf16[128,1152]{1,0:T(8,128)(2,1)S(1)} %collective-permute-done.24.refs_2_) | copy-start | bytes 884740
  284.8 13.5 %collective-permute-start.25 = (bf16[128,1152]{1,0:T(8,128)(2,1)S(1)}, bf16[128,1152]{1,0:T(8,128)(2,1)S(1)}, u32[]{:S(2)}, u32[]{:S(2)}) collective-permute-start(bf16[128,1152]{1,0:T(8,128)(2,1)S(1)} %collective-permute-done.24.refs_2_), channel_id=1, source_target_pairs={{0,8},{8,16},{16,24},{24,0},{1,9},{9,17},{17,25},{25,1},{2,10},{10... | collective-permute-start | bytes 884744 | tf_op jit(solution)/shard_map/ppermute | solution.py:449
  291.5 11.7 %copy-start.22 = (bf16[128,1152]{1,0:T(8,128)(2,1)}, bf16[128,1152]{1,0:T(8,128)(2,1)S(1)}, u32[]{:S(2)}) copy-start(bf16[128,1152]{1,0:T(8,128)(2,1)S(1)} %collective-permute-done.27.refs_6_) | copy-start | bytes 884740
  291.5 11.7 %collective-permute-start.28 = (bf16[128,1152]{1,0:T(8,128)(2,1)S(1)}, bf16[128,1152]{1,0:T(8,128)(2,1)S(1)}, u32[]{:S(2)}, u32[]{:S(2)}) collective-permute-start(bf16[128,1152]{1,0:T(8,128)(2,1)S(1)} %collective-permute-done.27.refs_6_), channel_id=1, source_target_pairs={{0,24},{8,0},{16,8},{24,16},{1,25},{9,1},{17,9},{25,17},{2,26},{10... | collective-permute-start | bytes 884744 | tf_op jit(solution)/shard_map/ppermute | solution.py:450
  307.6 5.7 %copy-start.32 = (bf16[48,1152]{1,0:T(8,128)(2,1)S(1)}, bf16[48,1152]{1,0:T(8,128)(2,1)}, u32[]{:S(2)}) copy-start(bf16[48,1152]{1,0:T(8,128)(2,1)} %get-tuple-element.170.refs_4_) | copy-start | bytes 331780
  308.7 33.2 %all-to-all-start.4 = ((bf16[8,128,1152]{2,1,0:T(8,128)(2,1)}), bf16[8,128,1152]{2,1,0:T(8,128)(2,1)S(1)}, u32[]{:S(2)}, u32[]{:S(2)}) async-start(bf16[8,128,1152]{2,1,0:T(8,128)(2,1)} %choose_pieces.3), calls=%async_computation.4 | async-start | bytes 4718592 | tf_op jit(solution)/shard_map/all_to_all | solution.py:453
  312.5 7.8 %collective-permute-start.35 = (bf16[48,1152]{1,0:T(8,128)(2,1)S(1)}, bf16[48,1152]{1,0:T(8,128)(2,1)S(1)}, u32[]{:S(2)}, u32[]{:S(2)}) collective-permute-start(bf16[48,1152]{1,0:T(8,128)(2,1)S(1)} %copy-done.31), channel_id=1, source_target_pairs={{0,8},{8,16},{16,24},{24,0},{1,9},{9,17},{17,25},{25,1},{2,10},{10... | collective-permute-start | bytes 331784 | tf_op jit(solution)/shard_map/ppermute | solution.py:449
  313.4 8.2 %collective-permute-start.38 = (bf16[48,1152]{1,0:T(8,128)(2,1)S(1)}, bf16[48,1152]{1,0:T(8,128)(2,1)S(1)}, u32[]{:S(2)}, u32[]{:S(2)}) collective-permute-start(bf16[48,1152]{1,0:T(8,128)(2,1)S(1)} %copy-done.32), channel_id=1, source_target_pairs={{0,24},{8,0},{16,8},{24,16},{1,25},{9,1},{17,9},{25,17},{2,26},{10... | collective-permute-start | bytes 331784 | tf_op jit(solution)/shard_map/ppermute | solution.py:450
  320.3 14.9 %copy-start.33 = (bf16[48,1152]{1,0:T(8,128)(2,1)}, bf16[48,1152]{1,0:T(8,128)(2,1)S(1)}, u32[]{:S(2)}) copy-start(bf16[48,1152]{1,0:T(8,128)(2,1)S(1)} %collective-permute-done.35.refs_1_) | copy-start | bytes 331780
  320.3 7.1 %collective-permute-start.36 = (bf16[48,1152]{1,0:T(8,128)(2,1)S(1)}, bf16[48,1152]{1,0:T(8,128)(2,1)S(1)}, u32[]{:S(2)}, u32[]{:S(2)}) collective-permute-start(bf16[48,1152]{1,0:T(8,128)(2,1)S(1)} %collective-permute-done.35.refs_1_), channel_id=1, source_target_pairs={{0,8},{8,16},{16,24},{24,0},{1,9},{9,17},{17,25},{25,1},{2,10},{10... | collective-permute-start | bytes 331784 | tf_op jit(solution)/shard_map/ppermute | solution.py:449
  321.6 13.6 %copy-start.34 = (bf16[48,1152]{1,0:T(8,128)(2,1)}, bf16[48,1152]{1,0:T(8,128)(2,1)S(1)}, u32[]{:S(2)}) copy-start(bf16[48,1152]{1,0:T(8,128)(2,1)S(1)} %collective-permute-done.38.refs_5_) | copy-start | bytes 331780
  321.6 7.7 %collective-permute-start.39 = (bf16[48,1152]{1,0:T(8,128)(2,1)S(1)}, bf16[48,1152]{1,0:T(8,128)(2,1)S(1)}, u32[]{:S(2)}, u32[]{:S(2)}) collective-permute-start(bf16[48,1152]{1,0:T(8,128)(2,1)S(1)} %collective-permute-done.38.refs_5_), channel_id=1, source_target_pairs={{0,24},{8,0},{16,8},{24,16},{1,25},{9,1},{17,9},{25,17},{2,26},{10... | collective-permute-start | bytes 331784 | tf_op jit(solution)/shard_map/ppermute | solution.py:450
  327.5 7.7 %copy-start.35 = (bf16[48,1152]{1,0:T(8,128)(2,1)}, bf16[48,1152]{1,0:T(8,128)(2,1)S(1)}, u32[]{:S(2)}) copy-start(bf16[48,1152]{1,0:T(8,128)(2,1)S(1)} %collective-permute-done.36.refs_2_) | copy-start | bytes 331780
  327.5 6.6 %collective-permute-start.37 = (bf16[48,1152]{1,0:T(8,128)(2,1)S(1)}, bf16[48,1152]{1,0:T(8,128)(2,1)S(1)}, u32[]{:S(2)}, u32[]{:S(2)}) collective-permute-start(bf16[48,1152]{1,0:T(8,128)(2,1)S(1)} %collective-permute-done.36.refs_2_), channel_id=1, source_target_pairs={{0,8},{8,16},{16,24},{24,0},{1,9},{9,17},{17,25},{25,1},{2,10},{10... | collective-permute-start | bytes 331784 | tf_op jit(solution)/shard_map/ppermute | solution.py:449
  329.2 6.0 %copy-start.36 = (bf16[48,1152]{1,0:T(8,128)(2,1)}, bf16[48,1152]{1,0:T(8,128)(2,1)S(1)}, u32[]{:S(2)}) copy-start(bf16[48,1152]{1,0:T(8,128)(2,1)S(1)} %collective-permute-done.39.refs_6_) | copy-start | bytes 331780
  329.3 5.9 %collective-permute-start.40 = (bf16[48,1152]{1,0:T(8,128)(2,1)S(1)}, bf16[48,1152]{1,0:T(8,128)(2,1)S(1)}, u32[]{:S(2)}, u32[]{:S(2)}) collective-permute-start(bf16[48,1152]{1,0:T(8,128)(2,1)S(1)} %collective-permute-done.39.refs_6_), channel_id=1, source_target_pairs={{0,24},{8,0},{16,8},{24,16},{1,25},{9,1},{17,9},{25,17},{2,26},{10... | collective-permute-start | bytes 331784 | tf_op jit(solution)/shard_map/ppermute | solution.py:450
  342.0 19.7 %all-to-all-start.6 = ((bf16[8,48,1152]{2,1,0:T(8,128)(2,1)}), bf16[8,48,1152]{2,1,0:T(8,128)(2,1)S(1)}, u32[]{:S(2)}, u32[]{:S(2)}) async-start(bf16[8,48,1152]{2,1,0:T(8,128)(2,1)} %choose_pieces.5), calls=%async_computation.6 | async-start | bytes 1769472 | tf_op jit(solution)/shard_map/all_to_all | solution.py:453
  (20 other events, 45.4 us)
